TPU v7x, 32 devices: a 4x2x2 block of a 4x4x8 slice. The times are simulated.
32 devices in a mesh: dp: 4 (over y, z), tp: 8 (over x, core).
Axes of the slice: x: 4, y: 2, z: 2, core: 2. Of those that a mesh axis runs over, the one named last changes fastest.
The devices are a block of a 4x4x8 slice.
Arguments:
- token_act: bfloat16 [64, 512, 768], P('dp'), parts along dimension 0
- token_cond: bfloat16 [64, 512, 384], P('dp'), parts along dimension 0
- pair_bias: bfloat16 [2, 16, 512, 512], P(None, 'tp')
- token_mask: int32 [512], replicated
- ada_scale: float32 [2, 2, 384], replicated
- ada_w: bfloat16 [2, 2, 384, 2, 768], replicated
- ada_bias: float32 [2, 2, 768], replicated
- zero_w: bfloat16 [2, 384, 2, 768], replicated
- zero_b: float32 [2, 2, 768], replicated
- w_qkvg: bfloat16 [2, 768, 4, 768], P(None, None, None, 'tp')
- b_q: float32 [2, 768], P(None, 'tp')
- w_o: bfloat16 [2, 768, 768], P(None, 'tp')
- w_up: bfloat16 [2, 768, 2, 1536], P(None, None, None, 'tp')
- w_down: bfloat16 [2, 1536, 768], P(None, 'tp')
Outputs:
- output: bfloat16 [64, 512, 768], P('dp'), parts along dimension 0
There are 4 independent parts. A program takes and returns all parts, laid end to end along the dimension named above; an argument that names none is the same for every part.
All inputs are finite; a program needn't handle non-finite values.
Results may differ from a plain program's by a relative error of at most 0.0181938.
Values are sent between devices in bfloat16 or wider.
A program may use at most 768 MiB of HBM per device.

v0:
```python
import math
import functools
import jax
import jax.numpy as jnp
from jax import lax
from jax.sharding import PartitionSpec as P

LN_EPS = 1e-5


def layer_norm(values_in):
    row_mean = jnp.mean(values_in, axis=-1, keepdims=True)
    centered = values_in - row_mean
    variance = jnp.mean(centered * centered, axis=-1, keepdims=True)
    return centered * lax.rsqrt(variance + LN_EPS)


def ada_norm(act_f32, cond_normed, scale_vec, weight, bias_vec):
    cond_in = (cond_normed * scale_vec).astype(jnp.bfloat16)
    modulation = jnp.einsum('rc,cgd->rgd', cond_in, weight, preferred_element_type=jnp.float32)
    return (jax.nn.sigmoid(modulation[:, 0] + bias_vec) * layer_norm(act_f32) + modulation[:, 1]).astype(jnp.bfloat16)


def attend_sample(bias_layer, mask_add, logit_scale, operands):
    query_one, key_one, value_one = operands
    logits = jnp.einsum('qhc,khc->hqk', query_one, key_one, preferred_element_type=jnp.float32) * logit_scale + bias_layer + mask_add
    attn_probs = jax.nn.softmax(logits, axis=-1).astype(jnp.bfloat16)
    return jnp.einsum('hqk,khc->qhc', attn_probs, value_one, preferred_element_type=jnp.float32)


def solution(mesh):
    def shard_body(token_act, token_cond, pair_bias, token_mask, ada_scale, ada_w, ada_bias, zero_w, zero_b, w_qkvg, b_q, w_o, w_up, w_down):
        samples, tokens, model_width = token_act.shape
        cond_dim = token_cond.shape[-1]
        heads_local = pair_bias.shape[1]
        local_width = w_qkvg.shape[-1]
        head_dim = local_width // heads_local
        row_count = samples * tokens
        head_shape = (samples, tokens, heads_local, head_dim)
        logit_scale = 1.0 / math.sqrt(head_dim)
        mask_add = (token_mask.astype(jnp.float32) - 1.0) * 1e9
        cond_flat = token_cond.reshape(row_count, cond_dim)
        cond_normed = layer_norm(cond_flat.astype(jnp.float32))
        act_flat = token_act.reshape(row_count, model_width)
        for layer_idx in range(pair_bias.shape[0]):
            out_gates = jax.nn.sigmoid(jnp.einsum('rc,cgd->rgd', cond_flat, zero_w[layer_idx], preferred_element_type=jnp.float32) + zero_b[layer_idx])
            act_f32 = act_flat.astype(jnp.float32)
            normed = ada_norm(act_f32, cond_normed, ada_scale[layer_idx, 0], ada_w[layer_idx, 0], ada_bias[layer_idx, 0])
            projected = jnp.einsum('rd,dfe->rfe', normed, w_qkvg[layer_idx], preferred_element_type=jnp.float32)
            query_rows = (projected[:, 0] + b_q[layer_idx]).astype(jnp.bfloat16).reshape(head_shape)
            key_rows = projected[:, 1].astype(jnp.bfloat16).reshape(head_shape)
            value_rows = projected[:, 2].astype(jnp.bfloat16).reshape(head_shape)
            gate_heads = jax.nn.sigmoid(projected[:, 3])
            attend_layer = functools.partial(attend_sample, pair_bias[layer_idx], mask_add, logit_scale)
            mixed_heads = lax.map(attend_layer, (query_rows, key_rows, value_rows)).reshape(row_count, local_width)
            heads_out = (gate_heads * mixed_heads).astype(jnp.bfloat16)
            attn_part = jnp.dot(heads_out, w_o[layer_idx], preferred_element_type=jnp.float32).astype(jnp.bfloat16)
            attn_out = lax.psum(attn_part, 'tp').astype(jnp.float32)
            mid_f32 = (act_f32 + out_gates[:, 0] * attn_out).astype(jnp.bfloat16).astype(jnp.float32)
            normed_mid = ada_norm(mid_f32, cond_normed, ada_scale[layer_idx, 1], ada_w[layer_idx, 1], ada_bias[layer_idx, 1])
            hidden_pre = jnp.einsum('rd,dgf->rgf', normed_mid, w_up[layer_idx], preferred_element_type=jnp.float32)
            hidden = (jax.nn.silu(hidden_pre[:, 0]) * hidden_pre[:, 1]).astype(jnp.bfloat16)
            trans_part = jnp.dot(hidden, w_down[layer_idx], preferred_element_type=jnp.float32).astype(jnp.bfloat16)
            trans_out = lax.psum(trans_part, 'tp').astype(jnp.float32)
            act_flat = (mid_f32 + out_gates[:, 1] * trans_out).astype(jnp.bfloat16)
        return act_flat.reshape(samples, tokens, model_width)

    everywhere = P()
    in_specs = (P('dp', None, None), P('dp', None, None), P(None, 'tp', None, None), P(None), everywhere, everywhere, everywhere, everywhere, everywhere, P(None, None, None, 'tp'), P(None, 'tp'), P(None, 'tp', None), P(None, None, None, 'tp'), P(None, 'tp', None))
    return jax.shard_map(shard_body, mesh=mesh, in_specs=in_specs, out_specs=P('dp', None, None), check_vma=False)
```

profile of v0, /device:TPU:81, one launch (start us, length us, event | category | flops | bytes accessed | tf_op | source)
XLA Modules:
  0.0 1142.5 jit_solution(4767125555497274213)
XLA Ops:
  7.5 4.4 convert_reduce_fusion.3
  14.9 4.2 fusion.191
  19.8 6.3 convert_reduce_fusion.4
  26.1 8.3 multiply_reduce_fusion
  35.4 11.5 %fusion.132 = (bf16[16,512,384]{2,1,0:T(8,128)(2,1)}, bf16[16,512,384]{2,1,0:T(8,128)(2,1)}, bf16[16,512,384]{2,1,0:T(8,128)(2,1)}, bf16[16,512,384]{2,1,0:T(8,128)(2,1)}) fusion(bf16[16,512,384]{2,1,0:T(8,128)(2,1)} %param.19, f32[384]{0:T(512)S(1)} %get-tuple-element.113, f32[16,512]{1,0:T(8,128)S(1)} %add_rsqrt_fusion.3, ...), kind=kLoop, calls=%fused_computation.135 | loop fusion | flops 34603008 | bytes 31528960 | tf_op jit(solution)/shard_map/convert_element_type | solution.py:19
  46.8 23.8 %fusion.161 = f32[8192,2,768]{2,0,1:T(8,128)} fusion(bf16[8192,384,1]{1,0,2:T(8,128)(2,1)} %bitcast.350, bf16[1,1,384,2,768]{4,3,2,1,0:T(2,128)(2,1)S(1)} %get-tuple-element.168), kind=kOutput, calls=%fused_computation.173 | convolution fusion | flops 9663676416 | bytes 57802752 | tf_op jit(solution)/shard_map/rc,cgd->rgd/dot_general | solution.py:20
  70.7 24.8 %fusion.113 = bf16[8192,1,768]{2,0,1:T(8,128)(2,1)} fusion(f32[8192,2,768]{2,0,1:T(8,128)} %fusion.161, bf16[16,512,768]{2,1,0:T(8,128)(2,1)} %param.18, f32[8192]{0:T(1024)S(1)} %bitcast.381, f32[8192]{0:T(1024)S(1)} %bitcast.382, f32[768]{0:T(1024)S(1)} %get-tuple-element.111), kind=kLoop, calls=%fused_computation.106 | loop fusion | flops 62914560 | bytes 75566080 | tf_op jit(solution)/shard_map/convert_element_type | solution.py:21
  95.5 8.3 fusion.134
  103.8 4.8 copy-done.1
  111.1 8.1 convert.10
  138.1 86.8 %while.20 = (s32[]{:T(128)}, f32[16,512,2,48]{1,3,2,0:T(8,128)}, bf16[16,512,2,48]{1,3,2,0:T(8,128)(2,1)}, bf16[16,512,2,48]{1,3,2,0:T(8,128)(2,1)}, bf16[16,512...) while((s32[]{:T(128)}, f32[16,512,2,48]{1,3,2,0:T(8,128)}, ...), condition=%wide.region_7.8_spmd, body=%wide.region_4.7_spmd.sunk | while | flops 157812736 | bytes 2800725 | solution.py:55
  140.5 3.2 fusion.228
  151.2 3.2 fusion.228
  162.0 3.2 fusion.228
  172.8 3.2 fusion.228
  183.6 3.2 fusion.228
  194.4 3.2 fusion.228
  205.2 3.2 fusion.228
  231.3 6.6 convolution_convert_fusion.1
  245.4 23.9 %fusion.160 = f32[8192,2,768]{2,0,1:T(8,128)} fusion(bf16[8192,384,1]{1,0,2:T(8,128)(2,1)} %bitcast.349, bf16[1,1,384,2,768]{4,3,2,1,0:T(2,128)(2,1)S(1)} %copy-done.9), kind=kOutput, calls=%fused_computation.171 | convolution fusion | flops 9663676416 | bytes 57802752 | tf_op jit(solution)/shard_map/rc,cgd->rgd/dot_general | solution.py:20
  269.3 29.6 %add_divide_fusion.1 = f32[8192,2,768]{2,0,1:T(8,128)} fusion(f32[2,768]{1,0:T(2,128)S(1)} %get-tuple-element.180, bf16[8192,384,1]{1,0,2:T(8,128)(2,1)} %bitcast.345, bf16[1,384,2,768]{3,2,1,0:T(2,128)(2,1)S(1)} %copy-done.15), kind=kOutput, calls=%fused_computation.47 | convolution fusion | flops 9714008064 | bytes 57808896 | tf_op jit(solution)/shard_map/rc,cgd->rgd/dot_general | solution.py:46
  298.9 80.6 %all-reduce.5.cloned.1.call-done = bf16[8192,768]{1,0:T(8,128)(2,1)} async-done(((bf16[8192,768]{1,0:T(8,128)(2,1)}), bf16[8192,768]{1,0:T(8,128)(2,1)}) %all-reduce.5.cloned.1.call-update) | async-done | bytes 12582928 | tf_op jit(solution)/shard_map/psum | solution.py:58
  379.5 22.2 %convert_reduce_fusion.2 = (f32[8192]{0:T(1024)S(1)}, bf16[8192,768]{1,0:T(8,128)(2,1)}) fusion(bf16[8192,768]{1,0:T(8,128)(2,1)} %all-reduce.5.cloned.1.call-done, f32[8192,2,768]{2,0,1:T(8,128)} %add_divide_fusion.1, bf16[16,512,768]{2,1,0:T(8,128)(2,1)} %param.18), kind=kLoop, calls=%fused_computation.56 | loop fusion | flops 44032000 | bytes 62947328 | tf_op jit(solution)/shard_map/reduce_sum | solution.py:12
  401.7 8.2 fusion.88
  409.9 26.8 %fusion.136 = f32[8192,384]{0,1} fusion(bf16[768,384]{0,1:T(8,128)(2,1)S(1)} %bitcast.379, bf16[8192,768]{1,0:T(8,128)(2,1)} %get-tuple-element.152, f32[8192,2,768]{2,0,1:T(8,128)} %fusion.160, f32[8192]{0:T(1024)S(1)} %add_rsqrt_fusion.2, f32[8192]{0:T(1024)S(1)} %broadcast_multiply_fusion.2, f32[768]{0:T(1024)S(1)} %copy-done.25), kind=kOutput, calls=%fused_computation.140 | convolution fusion | flops 4894752768 | bytes 76155904
  436.7 13.8 %convolution_convert_fusion.3 = bf16[8192,768]{1,0:T(8,128)(2,1)} fusion(f32[8192,2,192]{0,2,1:T(8,128)} %bitcast.383, bf16[2,192,768]{2,1,0:T(8,128)(2,1)S(1)} %copy-done.31), kind=kOutput, calls=%fused_computation.131 | convolution fusion | flops 2431647744 | bytes 25460736 | tf_op jit(solution)/shard_map/dot_general | solution.py:63
  453.3 23.8 %fusion.159 = f32[8192,2,768]{2,0,1:T(8,128)} fusion(bf16[8192,384,1]{1,0,2:T(8,128)(2,1)} %bitcast.348, bf16[1,1,384,2,768]{4,3,2,1,0:T(2,128)(2,1)S(1)} %copy-done.8), kind=kOutput, calls=%fused_computation.168 | convolution fusion | flops 9663676416 | bytes 57802752 | tf_op jit(solution)/shard_map/rc,cgd->rgd/dot_general | solution.py:20
  477.1 23.7 %fusion.158 = f32[8192,2,768]{2,0,1:T(8,128)} fusion(bf16[8192,384,1]{1,0,2:T(8,128)(2,1)} %bitcast.347, bf16[1,1,384,2,768]{4,3,2,1,0:T(2,128)(2,1)S(1)} %copy-done.7), kind=kOutput, calls=%fused_computation.166 | convolution fusion | flops 9663676416 | bytes 57802752 | tf_op jit(solution)/shard_map/rc,cgd->rgd/dot_general | solution.py:20
  500.9 87.3 %all-reduce.7.cloned.1.call-done = bf16[8192,768]{1,0:T(8,128)(2,1)} async-done(((bf16[8192,768]{1,0:T(8,128)(2,1)}), bf16[8192,768]{1,0:T(8,128)(2,1)}) %all-reduce.7.cloned.1.call-update) | async-done | bytes 12582928 | tf_op jit(solution)/shard_map/psum | solution.py:64
  588.1 21.8 %convert_reduce_fusion.1 = (f32[8192]{0:T(1024)S(1)}, bf16[8192,768]{1,0:T(8,128)(2,1)}) fusion(bf16[8192,768]{1,0:T(8,128)(2,1)} %all-reduce.7.cloned.1.call-done, f32[8192,2,768]{2,0,1:T(8,128)} %add_divide_fusion.1, bf16[8192,768]{1,0:T(8,128)(2,1)} %get-tuple-element.152), kind=kLoop, calls=%fused_computation.53 | loop fusion | flops 44032000 | bytes 62947328 | tf_op jit(solution)/shard_map/reduce_sum | solution.py:12
  609.9 8.2 fusion.84
  618.2 27.0 %fusion.138 = f32[8192,384]{0,1} fusion(bf16[768,384]{0,1:T(8,128)(2,1)S(1)} %bitcast.377, bf16[8192,768]{1,0:T(8,128)(2,1)} %get-tuple-element.150, f32[8192,2,768]{2,0,1:T(8,128)} %fusion.159, f32[8192]{0:T(1024)S(1)} %add_rsqrt_fusion.1, f32[8192]{0:T(1024)S(1)} %broadcast_multiply_fusion.1, f32[768]{0:T(1024)S(1)} %copy-done.24), kind=kOutput, calls=%fused_computation.141 | convolution fusion | flops 4894752768 | bytes 76155904
  645.2 5.5 convert.11
  650.7 5.4 fusion.146
  668.6 86.8 %while.21 = (s32[]{:T(128)}, f32[16,512,2,48]{1,3,2,0:T(8,128)}, bf16[16,512,2,48]{1,3,2,0:T(8,128)(2,1)}, bf16[16,512,2,48]{1,3,2,0:T(8,128)(2,1)}, bf16[16,512...) while((s32[]{:T(128)}, f32[16,512,2,48]{1,3,2,0:T(8,128)}, ...), condition=%wide.region_17.18_spmd, body=%wide.region_14.17_spmd.sunk | while | flops 157812736 | bytes 2800725 | solution.py:55
  676.4 3.2 fusion.235
  687.2 3.2 fusion.235
  708.8 3.2 fusion.235
  751.9 3.2 fusion.235
  761.8 6.4 convolution_convert_fusion
  769.4 29.7 %add_divide_fusion = f32[8192,2,768]{2,0,1:T(8,128)} fusion(f32[2,768]{1,0:T(2,128)S(1)} %copy-done.22, bf16[8192,384,1]{1,0,2:T(8,128)(2,1)} %bitcast.346, bf16[1,384,2,768]{3,2,1,0:T(2,128)(2,1)S(1)} %copy-done.14), kind=kOutput, calls=%fused_computation.46 | convolution fusion | flops 9714008064 | bytes 57808896 | tf_op jit(solution)/shard_map/rc,cgd->rgd/dot_general | solution.py:46
  799.1 106.6 %all-reduce.9.cloned.1.call-done = bf16[8192,768]{1,0:T(8,128)(2,1)} async-done(((bf16[8192,768]{1,0:T(8,128)(2,1)}), bf16[8192,768]{1,0:T(8,128)(2,1)}) %all-reduce.9.cloned.1.call-update) | async-done | bytes 12582928 | tf_op jit(solution)/shard_map/psum | solution.py:58
  905.7 21.8 %convert_reduce_fusion = (f32[8192]{0:T(1024)S(1)}, bf16[8192,768]{1,0:T(8,128)(2,1)}) fusion(bf16[8192,768]{1,0:T(8,128)(2,1)} %all-reduce.9.cloned.1.call-done, f32[8192,2,768]{2,0,1:T(8,128)} %add_divide_fusion, bf16[8192,768]{1,0:T(8,128)(2,1)} %get-tuple-element.150), kind=kLoop, calls=%fused_computation.50 | loop fusion | flops 44032000 | bytes 62947328 | tf_op jit(solution)/shard_map/reduce_sum | solution.py:12
  927.5 8.2 fusion.80
  935.8 27.0 %fusion.140 = f32[8192,384]{0,1} fusion(bf16[768,384]{0,1:T(8,128)(2,1)S(1)} %bitcast.378, bf16[8192,768]{1,0:T(8,128)(2,1)} %get-tuple-element.148, f32[8192,2,768]{2,0,1:T(8,128)} %fusion.158, f32[8192]{0:T(1024)S(1)} %add_rsqrt_fusion, f32[8192]{0:T(1024)S(1)} %broadcast_multiply_fusion, f32[768]{0:T(1024)S(1)} %copy-done.23), kind=kOutput, calls=%fused_computation.142 | convolution fusion | flops 4894752768 | bytes 76155904
  962.8 13.8 %convolution_convert_fusion.2 = bf16[8192,768]{1,0:T(8,128)(2,1)} fusion(f32[8192,2,192]{0,2,1:T(8,128)} %bitcast.384, bf16[2,192,768]{2,1,0:T(8,128)(2,1)S(1)} %copy-done.32), kind=kOutput, calls=%fused_computation.130 | convolution fusion | flops 2431647744 | bytes 25460736 | tf_op jit(solution)/shard_map/dot_general | solution.py:63
  976.7 137.5 %all-reduce.11.cloned.1.call-done = bf16[8192,768]{1,0:T(8,128)(2,1)} async-done(((bf16[8192,768]{1,0:T(8,128)(2,1)}), bf16[8192,768]{1,0:T(8,128)(2,1)}) %all-reduce.11.cloned.1.call-update) | async-done | bytes 12582928 | tf_op jit(solution)/shard_map/psum | solution.py:64
  1114.1 21.6 %fusion.94 = bf16[8192,768]{1,0:T(8,128)(2,1)} fusion(bf16[8192,768]{1,0:T(8,128)(2,1)} %get-tuple-element.148, f32[8192,2,768]{2,0,1:T(8,128)} %add_divide_fusion, bf16[8192,768]{1,0:T(8,128)(2,1)} %all-reduce.11.cloned.1.call-done), kind=kLoop, calls=%fused_computation.77 | loop fusion | flops 31457280 | bytes 62914560 | tf_op jit(solution)/shard_map/convert_element_type | solution.py:65
  (177 shorter events, 201.6 us)
Async XLA Ops:
  6.5 373.0 %all-reduce.5.cloned.1.call-start = ((), (), s32[]{:S(2)}) async-start(), calls=%async_computation | async-start | bytes 25165824 | tf_op jit(solution)/shard_map/psum | solution.py:58
  6.6 5.3 copy-start
  7.5 7.5 copy-start.6
  14.9 4.3 copy-start.20
  26.1 8.4 copy-start.13
  103.8 4.8 copy-start.1
  119.1 2.2 copy-start.29
  124.1 5.3 copy-start.12
  126.8 6.3 copy-start.26
  138.1 86.8 %copy-start.2 = (f32[8192,1,96]{0,2,1:T(8,128)S(1)}, f32[8192,1,96]{0,2,1:T(8,128)}, u32[]{:S(2)}) copy-start(f32[8192,1,96]{0,2,1:T(8,128)} %get-tuple-element.155) | copy-start | bytes 9437188
  224.9 4.5 copy-start.27
  224.9 2.3 copy-start.5
  227.2 4.1 copy-start.18
  237.9 1.7 copy-start.11
  237.9 4.8 copy-start.21
  238.0 7.4 copy-start.9
  238.0 350.1 %all-reduce.7.cloned.1.call-start = ((), (), s32[]{:S(2)}) async-start(), calls=%async_computation.1 | async-start | bytes 25165824 | tf_op jit(solution)/shard_map/psum | solution.py:64
  245.4 23.9 %copy-start.15 = (bf16[1,384,2,768]{3,2,1,0:T(2,128)(2,1)S(1)}, bf16[1,384,2,768]{3,2,1,0:T(2,128)(2,1)}, u32[]{:S(2)}) copy-start(bf16[1,384,2,768]{3,2,1,0:T(2,128)(2,1)} %get-tuple-element.170) | copy-start | bytes 3538948
  401.7 8.2 copy-start.25
  409.9 26.8 %copy-start.31 = (bf16[2,192,768]{2,1,0:T(8,128)(2,1)S(1)}, bf16[2,192,768]{2,1,0:T(8,128)(2,1)}, u32[]{:S(2)}) copy-start(bf16[2,192,768]{2,1,0:T(8,128)(2,1)} %param.31) | copy-start | bytes 1769476
  450.6 0.6 copy-start.30
  450.6 1.2 copy-start.10
  450.6 2.7 copy-start.8
  450.6 455.1 %all-reduce.9.cloned.1.call-start = ((), (), s32[]{:S(2)}) async-start(), calls=%async_computation.2 | async-start | bytes 25165824 | tf_op jit(solution)/shard_map/psum | solution.py:58
  453.3 23.9 %copy-start.7 = (bf16[1,1,384,2,768]{4,3,2,1,0:T(2,128)(2,1)S(1)}, bf16[1,1,384,2,768]{4,3,2,1,0:T(2,128)(2,1)}, u32[]{:S(2)}) copy-start(bf16[1,1,384,2,768]{4,3,2,1,0:T(2,128)(2,1)} %get-tuple-element.165) | copy-start | bytes 3538948
  609.9 8.3 copy-start.16
  609.9 8.3 copy-start.24
  661.5 7.1 copy-start.28
  668.6 86.8 %copy-start.3 = (f32[8192,1,96]{0,2,1:T(8,128)S(1)}, f32[8192,1,96]{0,2,1:T(8,128)}, u32[]{:S(2)}) copy-start(f32[8192,1,96]{0,2,1:T(8,128)} %get-tuple-element.153) | copy-start | bytes 9437188
  755.4 2.3 copy-start.4
  757.7 4.1 copy-start.19
  768.1 1.3 copy-start.14
  768.1 1.3 copy-start.22
  768.2 345.9 %all-reduce.11.cloned.1.call-start = ((), (), s32[]{:S(2)}) async-start(), calls=%async_computation.3 | async-start | bytes 25165824 | tf_op jit(solution)/shard_map/psum | solution.py:64
  927.5 8.3 copy-start.17
  927.5 8.3 copy-start.23
  935.8 27.0 %copy-start.32 = (bf16[2,192,768]{2,1,0:T(8,128)(2,1)S(1)}, bf16[2,192,768]{2,1,0:T(8,128)(2,1)}, u32[]{:S(2)}) copy-start(bf16[2,192,768]{2,1,0:T(8,128)(2,1)} %param.31) | copy-start | bytes 1769476
Sparse Core Ops, SparseCore 0:
  238.1 141.3 all-reduce.4
  450.8 137.3 all-reduce.6
  768.3 137.3 all-reduce.8
  976.8 137.3 all-reduce.10
where the time goes:
time: 1150 us; the launch traced here: 1140 us
  matrix products  457 us (40%)
  waiting for transfers between devices  412 us (36%)
  other arithmetic  202 us (18%)
  local copies, waits for them, and re-layouts  56.6 us (5%)
  between operations  13.9 us (1%)
    psum x2, waiting for transfers between devices, shard_body(): trans_out = lax.psum(trans_part, 'tp').astype(jnp.float32)  225 us
    psum x2, waiting for transfers between devices, shard_body(): attn_out = lax.psum(attn_part, 'tp').astype(jnp.float32)  187 us
    dot_general x32, matrix products, attend_sample(): jnp.einsum('hqk,khc->qhc', attn_probs, value_one, preferred_element_type=...  101 us
    dot_general x4, matrix products, ada_norm(): jnp.einsum('rc,cgd->rgd', cond_in, weight, preferred_element_type=jnp.flo...  95.3 us
    unnamed x4, matrix products  89.1 us
    reduce_sum x5, other arithmetic, layer_norm(): row_mean = jnp.mean(values_in, axis=-1, keepdims=True)  76.4 us
    sub x32, matrix products, attend_sample(): attn_probs = jax.nn.softmax(logits, axis=-1).astype(jnp.bfloat16)  71.7 us
    dot_general x2, matrix products, shard_body(): jnp.einsum('rc,cgd->rgd', cond_flat, zero_w[layer_idx], preferred_element...  59.2 us
  transfers between devices with their start and end apart: 4, of which 4 were waited for; matrix products, arithmetic and copies ran while one was open for 12% of the time, Pallas kernels for 0%

commit v1 on v0

v1 whole, which is shorter than its diff:
```python
import math
import jax
import jax.numpy as jnp
from jax import lax
from jax.sharding import PartitionSpec as P

LN_EPS = 1e-5


def layer_norm(values_in):
    row_mean = jnp.mean(values_in, axis=-1, keepdims=True)
    centered = values_in - row_mean
    variance = jnp.mean(centered * centered, axis=-1, keepdims=True)
    return centered * lax.rsqrt(variance + LN_EPS)


def ada_norm(act_f32, cond_normed, scale_vec, weight, bias_vec):
    cond_in = (cond_normed * scale_vec).astype(jnp.bfloat16)
    gain = jnp.dot(cond_in, weight[:, 0], preferred_element_type=jnp.float32)
    shift = jnp.dot(cond_in, weight[:, 1], preferred_element_type=jnp.float32)
    return (jax.nn.sigmoid(gain + bias_vec) * layer_norm(act_f32) + shift).astype(jnp.bfloat16)


def solution(mesh):
    tp = mesh.shape['tp']

    def shard_body(token_act, token_cond, pair_bias, token_mask, ada_scale, ada_w, ada_bias, zero_w, zero_b, w_qkvg, b_q, w_o, w_up, w_down):
        samples, tokens, model_width = token_act.shape
        cond_dim = token_cond.shape[-1]
        heads_local = pair_bias.shape[1]
        local_width = w_qkvg.shape[-1]
        head_dim = local_width // heads_local
        own = samples // tp
        me = lax.axis_index('tp')
        act_own = lax.dynamic_slice_in_dim(token_act, me * own, own, 0)
        cond_own = lax.dynamic_slice_in_dim(token_cond, me * own, own, 0)
        row_count = own * tokens
        logit_scale = 1.0 / math.sqrt(head_dim)
        mask_add = (token_mask.astype(jnp.float32) - 1.0) * 1e9
        cond_flat = cond_own.reshape(row_count, cond_dim)
        cond_normed = layer_norm(cond_flat.astype(jnp.float32))
        act_flat = act_own.reshape(row_count, model_width)
        for layer in range(pair_bias.shape[0]):
            qkvg_all = lax.all_gather(w_qkvg[layer].reshape(model_width, -1), 'tp')
            bias_all = lax.all_gather(pair_bias[layer], 'tp')
            wo_all = lax.all_gather(w_o[layer], 'tp', tiled=True)
            bq_all = lax.all_gather(b_q[layer], 'tp')
            up_all = lax.all_gather(w_up[layer].reshape(model_width, -1), 'tp')
            down_all = lax.all_gather(w_down[layer], 'tp')
            out_gates = [jax.nn.sigmoid(jnp.dot(cond_flat, zero_w[layer, :, j], preferred_element_type=jnp.float32) + zero_b[layer, j]) for j in range(2)]
            act_f32 = act_flat.astype(jnp.float32)
            normed = ada_norm(act_f32, cond_normed, ada_scale[layer, 0], ada_w[layer, 0], ada_bias[layer, 0])
            heads_out = []
            for t in range(tp):
                projected = jnp.dot(normed, qkvg_all[t], preferred_element_type=jnp.float32).reshape(own, tokens, 4, heads_local, head_dim)
                query = (projected[:, :, 0] + bq_all[t].reshape(heads_local, head_dim)).astype(jnp.bfloat16)
                key = projected[:, :, 1].astype(jnp.bfloat16)
                value = projected[:, :, 2].astype(jnp.bfloat16)
                gate = jax.nn.sigmoid(projected[:, :, 3])
                logits = jnp.einsum('sqhc,skhc->shqk', query, key, preferred_element_type=jnp.float32) * logit_scale + bias_all[t] + mask_add
                probs = jax.nn.softmax(logits, axis=-1).astype(jnp.bfloat16)
                mixed = jnp.einsum('shqk,skhc->sqhc', probs, value, preferred_element_type=jnp.float32)
                heads_out.append((gate * mixed).astype(jnp.bfloat16).reshape(row_count, local_width))
            heads_cat = jnp.concatenate(heads_out, axis=-1)
            attn_out = jnp.dot(heads_cat, wo_all, preferred_element_type=jnp.float32).astype(jnp.bfloat16).astype(jnp.float32)
            mid_f32 = (act_f32 + out_gates[0] * attn_out).astype(jnp.bfloat16).astype(jnp.float32)
            normed_mid = ada_norm(mid_f32, cond_normed, ada_scale[layer, 1], ada_w[layer, 1], ada_bias[layer, 1])
            total = jnp.zeros((row_count, model_width), jnp.float32)
            for t in range(tp):
                hidden_pre = jnp.dot(normed_mid, up_all[t], preferred_element_type=jnp.float32).reshape(row_count, 2, -1)
                hidden = (jax.nn.silu(hidden_pre[:, 0]) * hidden_pre[:, 1]).astype(jnp.bfloat16)
                total += jnp.dot(hidden, down_all[t], preferred_element_type=jnp.float32)
            trans_out = total.astype(jnp.bfloat16).astype(jnp.float32)
            act_flat = (mid_f32 + out_gates[1] * trans_out).astype(jnp.bfloat16)
        return lax.all_gather(act_flat.reshape(own, tokens, model_width), 'tp', tiled=True)

    everywhere = P()
    in_specs = (P('dp', None, None), P('dp', None, None), P(None, 'tp', None, None), P(None), everywhere, everywhere, everywhere, everywhere, everywhere, P(None, None, None, 'tp'), P(None, 'tp'), P(None, 'tp', None), P(None, None, None, 'tp'), P(None, 'tp', None))
    return jax.shard_map(shard_body, mesh=mesh, in_specs=in_specs, out_specs=P('dp', None, None), check_vma=False)
```

time: 1150 us -> 564 us (0.49)
  waiting for transfers between devices: 412 us -> 68.6 us
  matrix products: 457 us -> 200 us
  other arithmetic: 202 us -> 80.8 us
  local copies, waits for them, and re-layouts: 56.6 us -> 172 us
  blocking collectives: 0 us -> 20.6 us
    psum x4 -> x0, waiting for transfers between devices: 412 us -> none  [the longest x2 225 us: shard_body(): trans_out = lax.psum(trans_part, 'tp').astype(jnp.float32)]
    dot_general x42 -> x94, matrix products: 296 us -> 200 us  [the longest x16 44.6 us: shard_body(): jnp.dot(normed, qkvg_all[t], preferred_element_type=jnp.float32)]
    unnamed x4 -> x0, matrix products: 89.1 us -> none
    reduce_sum x5 -> x2, other arithmetic: 76.4 us -> 3.04 us  [layer_norm(): row_mean = jnp.mean(values_in, axis=-1, keepdims=True)]
    sub x32 -> x0, matrix products: 71.7 us -> none  [attend_sample(): attn_probs = jax.nn.softmax(logits, axis=-1).astype(jnp.bfloat16)]
    all_gather x0 -> x11, waiting for transfers between devices: none -> 66.1 us  [the longest x1 66.1 us: shard_body(): lax.all_gather(act_flat.reshape(own, tokens, model_width), 'tp', tiled=True)]
    dot_general x0 -> x36, local copies, waits for them, and re-layouts: none -> 65.5 us  [the longest x18 34.3 us: shard_body(): jnp.dot(normed_mid, up_all[t], preferred_element_type=jnp.float32)]
    convert_element_type x6 -> x0, other arithmetic: 56.5 us -> none  [the longest x1 24.8 us: ada_norm(): (jax.nn.sigmoid(modulation[:, 0] + bias_vec) * layer_norm(act_f32) + modu...]
  transfers between devices with their start and end apart: 4 -> 11, of which waited for: 4 -> 1; matrix products, arithmetic and copies ran while one was open for 12% -> 75% of each run, Pallas kernels for 0% -> 0%
where the time goes in v1:
time: 564 us; the launch traced here: 557 us
  matrix products  200 us (35%)
  local copies, waits for them, and re-layouts  172 us (30%)
  other arithmetic  80.8 us (14%)
  waiting for transfers between devices  68.6 us (12%)
  blocking collectives  20.6 us (4%)
  between operations  15.1 us (3%)
    all_gather x1, waiting for transfers between devices, shard_body(): lax.all_gather(act_flat.reshape(own, tokens, model_width), 'tp', tiled=True)  66.1 us
    sub x16, other arithmetic, shard_body(): probs = jax.nn.softmax(logits, axis=-1).astype(jnp.bfloat16)  53.2 us
    dot_general x16, matrix products, shard_body(): jnp.dot(normed, qkvg_all[t], preferred_element_type=jnp.float32)  44.6 us
    dot_general x16, matrix products, shard_body(): jnp.einsum('sqhc,skhc->shqk', query, key, preferred_element_type=jnp.floa...  43.8 us
    unnamed x244, local copies, waits for them, and re-layouts  40.2 us
    dot_general x18, local copies, waits for them, and re-layouts, shard_body(): jnp.dot(normed_mid, up_all[t], preferred_element_type=jnp.float32)  34.3 us
    add x16, local copies, waits for them, and re-layouts, shard_body(): jnp.einsum('sqhc,skhc->shqk', query, key, preferred_element_type=jnp.floa...  31.7 us
    dot_general x18, local copies, waits for them, and re-layouts, shard_body(): jnp.dot(normed, qkvg_all[t], preferred_element_type=jnp.float32)  31.2 us
  transfers between devices with their start and end apart: 11, of which 1 were waited for; matrix products, arithmetic and copies ran while one was open for 75% of the time, Pallas kernels for 0%

profile of v1, /device:TPU:81, one launch (start us, length us, event | category | flops | bytes accessed | tf_op | source)
XLA Modules:
  0.0 556.9 jit_solution(13375677293507502789)
XLA Ops:
  20.3 2.7 constant_dynamic-slice_fusion.1
  24.8 6.2 %fusion.476 = (bf16[1,1,384,2,768]{4,3,2,1,0:T(2,128)(2,1)}, bf16[1,1,384,2,768]{4,3,2,1,0:T(2,128)(2,1)}, bf16[1,1,384,2,768]{4,3,2,1,0:T(2,128)(2,1)}, bf16[1,1,384,2,768]{4,3,2,1,0:T(2,128)(2,1)S(1)}) fusion(bf16[2,2,384,2,768]{4,3,2,1,0:T(2,128)(2,1)} %param.19), kind=kLoop, calls=%fused_computation.730 | loop fusion | bytes 9437184 | tf_op jit(solution)/shard_map/slice | solution.py:67
  34.9 12.3 %all-gather.2 = f32[8,1,96]{2,1,0:T(1,128)S(1)} all-gather(f32[1,1,96]{2,1,0:T(1,128)S(1)} %get-tuple-element.108), channel_id=1, replica_groups=mesh['dp'=4,'tp'=8] {'tp'}, dimensions={0}, use_global_device_ids=true | all-gather | bytes 3456 | tf_op jit(solution)/shard_map/all_gather | solution.py:47
  47.2 8.4 %all-gather.3 = f32[8,1,96]{2,1,0:T(1,128)S(1)} all-gather(f32[1,1,96]{2,1,0:T(1,128)S(1)} %get-tuple-element.107), channel_id=1, replica_groups=mesh['dp'=4,'tp'=8] {'tp'}, dimensions={0}, use_global_device_ids=true | all-gather | bytes 3456 | tf_op jit(solution)/shard_map/all_gather | solution.py:47
  56.3 4.8 fusion.477
  72.2 2.7 fusion.251
  74.9 2.6 fusion.250
  77.5 2.6 fusion.249
  80.2 2.8 fusion.42
  83.0 4.0 slice_bitcast_fusion.52
  91.2 3.9 fusion.497
  99.5 3.8 fusion.493
  105.4 3.7 fusion.491
  110.1 3.8 fusion.489
  114.2 3.6 fusion.487
  118.1 3.7 fusion.485
  122.0 3.7 fusion.483
  125.7 4.1 slice_bitcast_fusion.40
  142.6 4.0 slice_bitcast_fusion.28
  159.5 4.5 slice_bitcast_fusion.16
  176.9 3.7 fusion.409
  180.6 3.8 fusion.407
  184.4 3.9 fusion.405
  188.3 3.8 fusion.403
  192.0 3.8 fusion.401
  195.8 3.8 fusion.399
  199.6 3.7 fusion.397
  203.3 3.8 fusion.395
  207.2 9.7 %fusion.225 = (f32[2,512,512]{2,1,0:T(8,128)}, f32[2,512,512]{2,1,0:T(8,128)}, f32[2,512,512]{2,1,0:T(8,128)}, f32[2,512,512]{2,1,0:T(8,128)}, f32[2,512,512]{2,...) fusion(bf16[8,2,512,512]{3,2,1,0:T(8,128)(2,1)} %all-gather.18.cloned.1.call-done), kind=kLoop, calls=%fused_computation.305 | loop fusion | flops 4194304 | bytes 25165824 | tf_op jit(solution)/shard_map/add | solution.py:60
  218.8 5.0 fusion.498
  227.9 5.0 fusion.496
  236.7 5.0 fusion.494
  245.6 5.0 fusion.492
  255.1 5.0 fusion.490
  264.9 5.0 fusion.488
  274.4 5.0 fusion.486
  283.9 5.0 fusion.484
  296.5 3.3 convolution_convert_fusion.1
  319.1 2.3 fusion.369
  331.9 3.3 convert_reduce_fusion.1
  337.2 9.7 %fusion.217 = (f32[2,512,512]{2,1,0:T(8,128)}, f32[2,512,512]{2,1,0:T(8,128)}, f32[2,512,512]{2,1,0:T(8,128)}, f32[2,512,512]{2,1,0:T(8,128)}, f32[2,512,512]{2,...) fusion(bf16[8,2,512,512]{3,2,1,0:T(8,128)(2,1)} %all-gather.26.cloned.1.call-done), kind=kLoop, calls=%fused_computation.289 | loop fusion | flops 4194304 | bytes 25165824 | tf_op jit(solution)/shard_map/add | solution.py:60
  348.9 4.2 fusion.29
  369.4 2.3 copy.265
  433.9 3.3 convolution_convert_fusion
  456.4 2.3 fusion.354
  469.2 4.4 fusion.36
  473.6 66.1 %all-gather.32.cloned.1.call-done = bf16[16,512,768]{2,1,0:T(8,128)(2,1)} async-done(((bf16[2,512,768]{2,1,0:T(8,128)(2,1)}), bf16[16,512,768]{2,1,0:T(8,128)(2,1)}) %all-gather.32.cloned.1.call-update) | async-done | bytes 12582928 | tf_op jit(solution)/shard_map/all_gather | solution.py:75
  539.7 10.4 %copy.368 = bf16[16,512,768]{2,1,0:T(8,128)(2,1)} copy(bf16[16,512,768]{2,1,0:T(8,128)(2,1)} %all-gather.32.cloned.1.call-done) | data formatting | bytes 25165824
  (464 shorter events, 262.1 us)
Async XLA Ops:
  6.5 76.4 %all-gather.16.cloned.1.call-start = ((), (), s32[]{:S(2)}) async-start(), calls=%async_computation | async-start | bytes 5308416 | tf_op jit(solution)/shard_map/all_gather | solution.py:44
  9.1 116.6 %all-gather.20.cloned.1.call-start = ((), (), s32[]{:S(2)}) async-start(), calls=%async_computation.2 | async-start | bytes 5308416 | tf_op jit(solution)/shard_map/all_gather | solution.py:48
  10.4 132.2 %all-gather.24.cloned.1.call-start = ((), (), s32[]{:S(2)}) async-start(), calls=%async_computation.4 | async-start | bytes 5308416 | tf_op jit(solution)/shard_map/all_gather | solution.py:44
  11.6 147.9 %all-gather.28.cloned.1.call-start = ((), (), s32[]{:S(2)}) async-start(), calls=%async_computation.6 | async-start | bytes 5308416 | tf_op jit(solution)/shard_map/all_gather | solution.py:48
  12.8 194.4 %all-gather.18.cloned.1.call-start = ((), (), s32[]{:S(2)}) async-start(), calls=%async_computation.1 | async-start | bytes 9437184 | tf_op jit(solution)/shard_map/all_gather | solution.py:45
  14.4 282.1 %all-gather.34.cloned.1.call-start = ((), (), s32[]{:S(2)}) async-start(), calls=%async_computation.9 | async-start | bytes 1327104 | tf_op jit(solution)/shard_map/all_gather | solution.py:46
  15.3 303.9 %all-gather.22.cloned.1.call-start = ((), (), s32[]{:S(2)}) async-start(), calls=%async_computation.3 | async-start | bytes 2654208 | tf_op jit(solution)/shard_map/all_gather | solution.py:49
  16.3 321.0 %all-gather.26.cloned.1.call-start = ((), (), s32[]{:S(2)}) async-start(), calls=%async_computation.5 | async-start | bytes 9437184 | tf_op jit(solution)/shard_map/all_gather | solution.py:45
  17.1 416.8 %all-gather.36.cloned.1.call-start = ((), (), s32[]{:S(2)}) async-start(), calls=%async_computation.10 | async-start | bytes 1327104 | tf_op jit(solution)/shard_map/all_gather | solution.py:46
  17.9 438.5 %all-gather.30.cloned.1.call-start = ((), (), s32[]{:S(2)}) async-start(), calls=%async_computation.7 | async-start | bytes 2654208 | tf_op jit(solution)/shard_map/all_gather | solution.py:49
  18.5 521.2 %all-gather.32.cloned.1.call-start = ((), (), s32[]{:S(2)}) async-start(), calls=%async_computation.8 | async-start | bytes 14155776 | tf_op jit(solution)/shard_map/all_gather | solution.py:75
  20.3 4.5 copy-start.78
  31.0 3.3 copy-start.76
  31.0 3.9 copy-start.94
  31.0 24.7 %copy-start.93 = (s32[512]{0:T(512)S(1)}, s32[512]{0:T(512)}, u32[]{:S(2)}) copy-start(s32[512]{0:T(512)} %param.17) | copy-start | bytes 6148
  31.1 25.2 %copy-start = (bf16[2,384,2,768]{3,2,1,0:T(2,128)(2,1)S(1)}, bf16[2,384,2,768]{3,2,1,0:T(2,128)(2,1)}, u32[]{:S(2)}) copy-start(bf16[2,384,2,768]{3,2,1,0:T(2,128)(2,1)} %param.21) | copy-start | bytes 7077892
  56.3 4.8 copy-start.77
  56.3 5.4 copy-start.3
  61.1 8.2 %copy-start.1 = (bf16[1,1,384,2,768]{4,3,2,1,0:T(2,128)(2,1)S(1)}, bf16[1,1,384,2,768]{4,3,2,1,0:T(2,128)(2,1)}, u32[]{:S(2)}) copy-start(bf16[1,1,384,2,768]{4,3,2,1,0:T(2,128)(2,1)} %get-tuple-element.59) | copy-start | bytes 3538948
  69.4 8.2 %copy-start.11 = (bf16[1,1,384,2,768]{4,2,3,1,0:T(8,128)(2,1)}, bf16[1,1,384,2,768]{4,2,3,1,0:T(8,128)(2,1)S(1)}, u32[]{:S(2)}) copy-start(bf16[1,1,384,2,768]{4,2,3,1,0:T(8,128)(2,1)S(1)} %copy.349) | copy-start | bytes 3538948
  70.0 4.9 copy-start.9
  70.0 4.9 copy-start.8
  70.0 7.5 %copy-start.6 = (bf16[2,512,384]{2,1,0:T(8,128)(2,1)}, bf16[2,512,384]{2,1,0:T(8,128)(2,1)S(1)}, u32[]{:S(2)}) copy-start(bf16[2,512,384]{2,1,0:T(8,128)(2,1)S(1)} %get-tuple-element.97) | copy-start | bytes 2359300
  91.2 3.9 copy-start.72
  91.2 3.9 copy-start.102
  289.0 3.4 copy-start.60
  289.0 4.1 copy-start.58
  289.0 4.7 copy-start.57
  296.5 3.3 copy-start.51
  296.5 3.3 copy-start.53
  304.5 3.9 copy-start.27
  306.4 3.9 copy-start.28
  308.4 4.0 copy-start.29
  310.4 4.0 copy-start.30
  312.4 4.0 copy-start.31
  348.9 4.3 copy-start.71
  353.1 4.1 copy-start.95
  426.3 3.4 copy-start.59
  426.3 4.1 copy-start.56
  426.4 4.7 copy-start.55
  433.9 3.4 copy-start.47
  433.9 3.4 copy-start.89
  433.9 3.4 copy-start.52
  441.7 3.9 copy-start.19
  443.7 3.9 copy-start.20
  445.6 3.9 copy-start.21
  447.6 3.9 copy-start.22
  449.6 4.0 copy-start.23
  (66 other events, 142.7 us)
Sparse Core Ops, SparseCore 0:
  9.2 35.3 all-gather.15
  46.2 30.8 all-gather.19
  78.7 30.8 all-gather.23
  111.1 30.8 all-gather.27
  143.5 46.4 all-gather.17
  191.5 20.4 all-gather.33
  213.5 22.6 all-gather.21
  237.8 46.8 all-gather.25
  286.3 20.4 all-gather.35
  308.2 22.6 all-gather.29
  473.7 65.9 all-gather.31

commit v2 on v0

v2 whole, which is shorter than its diff:
```python
import functools
import math
import jax
import jax.numpy as jnp
from jax import lax
from jax.experimental import pallas as pl
from jax.experimental.pallas import tpu as pltpu
from jax.sharding import PartitionSpec as P

LN_EPS = 1e-5
LOG2E = 1.4426950408889634
MESH = pl.DeviceIdType.MESH
BF16 = jnp.bfloat16
F32 = jnp.float32
LANES = 128
CH = 1056
LA = 4
LAGS = (0, 1, 2, 3)
RB = 256
QB = 256
OUT_ROWS = 256
CORES = 2


def dot_nt(lhs, rhs):
    return lax.dot_general(lhs, rhs, (((1,), (1,)), ((), ())), preferred_element_type=F32)


def dot_nn(lhs, rhs):
    return lax.dot_general(lhs, rhs, (((1,), (0,)), ((), ())), preferred_element_type=F32)


def normed(values_in):
    row_mean = jnp.mean(values_in, axis=-1, keepdims=True)
    centered = values_in - row_mean
    variance = jnp.mean(centered * centered, axis=-1, keepdims=True)
    return centered * lax.rsqrt(variance + LN_EPS)


class Geometry:
    def __init__(self, mesh, act, cond, bias, w_qkvg, w_up):
        self.nx = mesh.shape['tp'] // CORES
        self.y_stride = len({d.coords[2] for d in mesh.devices.flat})
        self.samples, self.tokens, self.width = act
        self.cond_dim = cond[-1]
        self.layers, self.heads = bias[0], bias[1]
        self.lw = w_qkvg[-1]
        self.hd = self.lw // self.heads
        self.hu = w_up[-1]
        self.own = self.samples // mesh.shape['tp']
        self.ncol = self.width // LANES
        self.tcol = self.tokens // LANES
        self.q0 = 0
        self.b0 = self.q0 + self.ncol * 4 * self.lw
        self.o0 = self.b0 + self.heads * self.tcol * self.tokens
        self.u0 = self.o0 + self.ncol * self.lw
        self.d0 = self.u0 + self.ncol * 2 * self.hu
        self.lr = self.d0 + self.ncol * self.hu
        self.chunks = -(-self.layers * self.lr // CH)
        self.rows = self.chunks * CH
        self.per_layer = self.lr // CH + 1
        assert self.lw == 96 and self.hu == 192 and self.heads == 2 and self.nx == 4


def kernel(g, act_in, cond_in, bias_in, mask_in, ascale_in, ada_in, abias_in, zero_in, zbias_in, wq_in, bq_in, wo_in, up_in, down_in,
           out, buf, xbuf, pbuf, sbuf, obuf, hbuf, cbuf, lnbuf, adabuf, zerobuf, bqbuf, bmbuf, qbuf, kbuf, vbuf, gbuf,
           s_loc, s_act, s_ada, send, ra, rb, rc, rd, s_bq, r_bq, sx, rx, sp, rp, osend, o_p0, o_a, o_p1, o_d, o_p2):
    nx, own, T, D = g.nx, g.own, g.tokens, g.width
    tp = lax.axis_index('tp')
    dp = lax.axis_index('dp')
    x = tp // CORES
    c = lax.rem(tp, CORES)
    xp = lax.rem(x + 1, nx)
    xm = lax.rem(x + nx - 1, nx)
    xo = lax.rem(x + 2, nx)
    dev_p, dev_m, dev_o = ({'tp': v * CORES + c} for v in (xp, xm, xo))
    dev_c = {'tp': x * CORES + 1 - c}
    pz = lax.rem(dp, 2)
    py = lax.rem(dp // g.y_stride, 2)
    dev_z = {'dp': dp + 1 - 2 * pz}
    dev_y = {'dp': dp + g.y_stride * (1 - 2 * py)}

    def remote(src, dst, s_sem, r_sem, dev):
        return pltpu.make_async_remote_copy(src, dst, s_sem, r_sem, device_id=dev, device_id_type=MESH)

    def wait_like(ref, sem):
        pltpu.make_async_copy(ref, ref, sem).wait()

    lw, hu = g.lw, g.hu
    half = hu - LANES
    q_parts = ((0, 0, lw, 0), (3, 0, 32, lw), (1, 0, lw, LANES), (3, 32, 32, LANES + lw), (2, 0, lw, 2 * LANES), (3, 64, 32, 2 * LANES + lw))
    u_parts = ((0, 0, LANES, 0), (0, LANES, half, LANES), (1, LANES, half, LANES + half), (1, 0, LANES, 2 * LANES))

    def load_layer(l):
        def put(src, off, n):
            pltpu.make_async_copy(src, buf.at[x, pl.ds(l * g.lr + off, n)], s_loc.at[l]).start()
        for j in range(g.ncol):
            col = pl.ds(j * LANES, LANES)
            for f, r0, n, off in q_parts:
                put(wq_in.at[l, f, pl.ds(r0, n), col], g.q0 + j * 4 * lw + off, n)
        for h in range(g.heads):
            for j in range(g.tcol):
                put(bias_in.at[l, h, :, pl.ds(j * LANES, LANES)], g.b0 + (h * g.tcol + j) * T, T)
        for j in range(g.ncol):
            col = pl.ds(j * LANES, LANES)
            put(wo_in.at[l, :, col], g.o0 + j * lw, lw)
            for f, r0, n, off in u_parts:
                put(up_in.at[l, f, pl.ds(r0, n), col], g.u0 + j * 2 * hu + off, n)
            put(down_in.at[l, :, col], g.d0 + j * hu, hu)

    load_layer(0)
    mine = tp * own
    act_cp = pltpu.make_async_copy(act_in.at[pl.ds(mine, own)], out.at[pl.ds(mine, own)], s_act.at[0])
    cond_cp = pltpu.make_async_copy(cond_in.at[pl.ds(mine, own)], cbuf, s_act.at[1])
    ada_cp = pltpu.make_async_copy(ada_in, adabuf, s_ada.at[0])
    zero_cp = pltpu.make_async_copy(zero_in, zerobuf, s_ada.at[1])
    bq_cp = pltpu.make_async_copy(bq_in, bqbuf.at[x], s_act.at[2])
    for cp in (act_cp, cond_cp, bq_cp, ada_cp, zero_cp):
        cp.start()
    for l in range(1, g.layers):
        load_layer(l)

    barrier = pltpu.get_barrier_semaphore()
    devs = (dev_p, dev_m, dev_o, dev_c, dev_z, dev_y)
    for d in devs:
        pl.semaphore_signal(barrier, inc=1, device_id=d, device_id_type=MESH)
    pad = g.rows - g.layers * g.lr
    if pad:
        buf[x, pl.ds(g.layers * g.lr, pad), :] = jnp.zeros((pad, LANES), BF16)
    pl.semaphore_wait(barrier, len(devs))
    for l in range(g.layers):
        wait_like(buf.at[x, pl.ds(l * g.lr, g.lr)], s_loc.at[l])

    Q = CH // 4
    g0 = 2 * py + pz
    gy = 2 * (1 - py) + pz
    gz = 2 * py + 1 - pz
    gd = 2 * (1 - py) + 1 - pz

    def piece(blk, k, part):
        return buf.at[blk, pl.ds(pl.multiple_of(k * CH + part * Q, 8), Q)]

    def push(blk, k, part, dev, r_sem):
        r = piece(blk, k, part)
        remote(r, r, send, r_sem, dev).start()

    def await_quarters(n, sem):
        wait_like(buf.at[0, pl.ds(0, n * Q)], sem)

    def first(k):
        push(x, k, g0, dev_p, ra.at[k])
        push(x, k, g0, dev_m, ra.at[k])

    def stage1(k):
        await_quarters(2, ra.at[k])
        push(xm, k, g0, dev_p, rd.at[k])
        for blk in (xm, xp):
            push(blk, k, g0, dev_y, rb.at[k])
            push(blk, k, g0, dev_z, rb.at[k])

    def stage2(k):
        await_quarters(4, rb.at[k])
        push(xm, k, gy, dev_p, rd.at[k])
        push(xp, k, gz, dev_m, rd.at[k])
        push(xm, k, gz, dev_y, rc.at[k])
        push(xp, k, gy, dev_z, rc.at[k])

    def stage3(k):
        await_quarters(2, rc.at[k])
        push(xp, k, gd, dev_m, rd.at[k])

    def stage4(k):
        await_quarters(4, rd.at[k])

    K = g.chunks
    last_tick = K + LAGS[-1]

    def tick(t):
        @pl.when(t + LA < K)
        def _():
            first(t + LA)
        for lag, stage in zip(LAGS, (stage1, stage2, stage3, stage4)):
            @pl.when((t >= lag) & (t - lag < K))
            def _(lag=lag, stage=stage):
                stage(t - lag)

    def ahead(k, carry):
        first(k)
        return carry
    lax.fori_loop(0, LA, ahead, 0)

    carried = max(0, -(-g.lr // CH) + LAGS[-1] - g.per_layer)

    def reached(l, rel):
        return jnp.minimum(jnp.maximum(l * g.per_layer + rel, jnp.where(l > 0, l * g.per_layer + carried, 0)), last_tick)

    def advance(l, lo, hi):
        def body(t, carry):
            tick(t)
            return carry
        lax.fori_loop(reached(l, lo), reached(l, hi), body, 0)

    def need(rows_end, lag):
        return -(-rows_end // CH) + lag

    bq_cp.wait()
    for d in (dev_p, dev_m, dev_o):
        remote(bqbuf.at[x], bqbuf.at[x], s_bq, r_bq, d).start()
    act_cp.wait()
    cond_cp.wait()

    lane = lax.broadcasted_iota(jnp.int32, (1, LANES), 1)
    hd = g.hd
    mask_add = (mask_in[...].astype(F32) - 1.0) * (1e9 * LOG2E)
    scale2 = LOG2E / math.sqrt(hd)

    def cond_rows(i, r):
        rows = pl.ds(r * RB, RB)
        lnbuf[i, rows, :] = normed(cbuf[i, rows, :].astype(F32))

    nrb = T // RB
    for i in range(own):
        for r in range(nrb):
            cond_rows(i, r)
    ada_cp.wait()
    zero_cp.wait()

    def ada_rows(l, j, i, r):
        rows = pl.ds(pl.multiple_of(r * RB, RB), RB)
        lj = l * 2 + j
        c_in = (lnbuf[i, rows, :] * ascale_in[lj]).astype(BF16)
        gain = jax.nn.sigmoid(dot_nn(c_in, adabuf[lj, 0]) + abias_in[lj])
        shift = dot_nn(c_in, adabuf[lj, 1])
        xbuf[i, rows, :] = (gain * normed(out[mine + i, rows, :].astype(F32)) + shift).astype(BF16)

    def ada_sample(l, j, i):
        def body(r, carry):
            ada_rows(l, j, i, r)
            return carry
        lax.fori_loop(0, nrb, body, 0)
        remote(xbuf.at[i], xbuf.at[own + i], sx.at[i], rx.at[i], dev_c).start()

    def resid_rows(l, j, i, r, part_of):
        rows = pl.ds(pl.multiple_of(r * RB, RB), RB)
        lj = l * 2 + j
        total = (part_of(l, i, rows) + pbuf[i, rows, :].astype(F32)).astype(BF16).astype(F32)
        gate = jax.nn.sigmoid(dot_nn(cbuf[i, rows, :], zerobuf[lj]) + zbias_in[lj])
        out[mine + i, rows, :] = (out[mine + i, rows, :].astype(F32) + gate * total).astype(BF16)

    def resid_sample(l, j, i, part_of):
        wait_like(pbuf.at[i], rp.at[i])
        def body(r, carry):
            resid_rows(l, j, i, r, part_of)
            return carry
        lax.fori_loop(0, nrb, body, 0)

    def part_sample(l, i, part_of):
        def body(r, carry):
            rows = pl.ds(pl.multiple_of(r * RB, RB), RB)
            sbuf[i, rows, :] = part_of(l, own + i, rows).astype(BF16)
            return carry
        lax.fori_loop(0, nrb, body, 0)
        remote(sbuf.at[i], pbuf.at[i], sp.at[i], rp.at[i], dev_c).start()

    def flat(s, l, off, n):
        return buf[s, pl.ds(pl.multiple_of(l * g.lr + off, 8), n), :]

    def bias_prep(l, s):
        for h in range(g.heads):
            for j in range(g.tcol):
                col = pl.ds(j * LANES, LANES)
                bmbuf[h, :, col] = flat(s, l, g.b0 + (h * g.tcol + j) * T, T).astype(F32) * LOG2E + mask_add[:, j * LANES:(j + 1) * LANES]

    def unit(l, s, i):
        w = jnp.concatenate([flat(s, l, g.q0 + j * 4 * lw, 4 * lw) for j in range(g.ncol)], axis=1)
        for r in range(T // QB):
            rows = pl.ds(r * QB, QB)
            proj = dot_nt(xbuf[i, rows, :], w)
            pa, pb, pc = (proj[:, v * LANES:(v + 1) * LANES] for v in range(3))
            qbuf[rows, :] = (pa + bqbuf[s, pl.ds(l, 1), :]).astype(BF16)
            kbuf[rows, :] = pb.astype(BF16)
            vbuf[rows, :] = jnp.where(lane < lw, pc, 1.0).astype(BF16)
            gate = jnp.where(lane < 32, pltpu.roll(pa, 32, 1), jnp.where(lane < 64, pltpu.roll(pb, 64, 1), pltpu.roll(pc, 96, 1)))
            gbuf[rows, :] = jnp.where(lane < lw, jax.nn.sigmoid(gate), 0.0)
        keys = kbuf[...]
        values = vbuf[...]
        for r in range(T // QB):
            rows = pl.ds(r * QB, QB)
            mixed = []
            for h in range(g.heads):
                q = jnp.where((lane >= h * hd) & (lane < (h + 1) * hd), qbuf[rows, :], jnp.zeros((), BF16))
                z = dot_nt(q, keys) * scale2 + bmbuf[h, rows, :]
                e = jnp.exp2(z - jnp.max(z, axis=-1, keepdims=True)).astype(BF16)
                o = dot_nn(e, values)
                mixed.append(o * (1.0 / o[:, lw:lw + 1]))
            obuf[i, s, rows, :] = (jnp.where(lane < hd, mixed[0], mixed[1]) * gbuf[rows, :]).astype(BF16)

    def attend(l, s, lo, hi):
        def body(i, carry):
            unit(l, s, i)
            return carry
        lax.fori_loop(lo, hi, body, 0)

    def attn_part(l, i, rows):
        lhs = jnp.concatenate([obuf[i, s, rows, :] for s in range(nx)], axis=1)
        zpad = jnp.zeros((LANES - lw, LANES), BF16)
        rhs = jnp.concatenate([jnp.concatenate([v for s in range(nx) for v in (flat(s, l, g.o0 + j * lw, lw), zpad)], axis=0) for j in range(g.ncol)], axis=1)
        return dot_nn(lhs, rhs)

    def up_sample(l, i):
        for r in range(T // RB):
            rows = pl.ds(r * RB, RB)
            y = xbuf[i, rows, :]
            for p in range(nx // 2):
                mids = []
                for e in range(2):
                    s = 2 * p + e
                    w = jnp.concatenate([flat(s, l, g.u0 + j * 2 * hu, 2 * hu) for j in range(g.ncol)], axis=1)
                    u = dot_nt(y, w)
                    ua, ub, uc = (u[:, v * LANES:(v + 1) * LANES] for v in range(3))
                    side = (3 * p + 2 * e) * LANES
                    hbuf[i, rows, side:side + LANES] = (jax.nn.silu(ua) * uc).astype(BF16)
                    act = jax.nn.silu(ub)
                    mids.append(act * pltpu.roll(ub, half, 1) if e == 0 else pltpu.roll(act, half, 1) * ub)
                mid = (3 * p + 1) * LANES
                hbuf[i, rows, mid:mid + LANES] = jnp.where(lane < half, mids[0], mids[1]).astype(BF16)

    def trans_part(l, i, rows):
        cols = []
        for j in range(g.ncol):
            v = []
            for p in range(nx // 2):
                v.append(flat(2 * p, l, g.d0 + j * hu, hu))
                v.append(flat(2 * p + 1, l, g.d0 + j * hu + LANES, half))
                v.append(flat(2 * p + 1, l, g.d0 + j * hu, LANES))
            cols.append(jnp.concatenate(v, axis=0))
        return dot_nn(hbuf[i, rows, :], jnp.concatenate(cols, axis=1))

    def sends_done(ref, sem):
        for i in range(own):
            wait_like(ref.at[i], sem.at[i])

    t_q = need(g.b0, LAGS[2])
    t_near = need(g.o0, LAGS[2])
    t_far = need(g.u0, LAGS[3])
    t_up = need(g.d0, LAGS[3])
    t_down = need(g.lr, LAGS[3])

    def layer(l, carry):
        ada_sample(l, 0, 0)
        advance(l, 0, 1)
        ada_sample(l, 0, 1)
        advance(l, 1, 2)
        bias_prep(l, x)
        attend(l, x, 0, own)
        advance(l, 2, 3)
        for i in range(own):
            wait_like(xbuf.at[own + i], rx.at[i])
        attend(l, x, own, 2 * own)
        advance(l, 3, t_near)

        @pl.when(l == 0)
        def _():
            wait_like(bqbuf.at[pl.ds(0, nx - 1)], r_bq)
        bias_prep(l, xm)
        attend(l, xm, 0, 2 * own)
        advance(l, t_near, t_near + 1)
        bias_prep(l, xp)
        attend(l, xp, 0, 2 * own)
        advance(l, t_near + 1, t_far)
        bias_prep(l, xo)
        attend(l, xo, 0, 2 * own)
        sends_done(xbuf, sx)
        for i in range(own):
            part_sample(l, i, attn_part)
        for i in range(own):
            resid_sample(l, 0, i, attn_part)
        for i in range(own):
            ada_sample(l, 1, i)
        sends_done(sbuf, sp)
        advance(l, t_far, t_up)
        def up_body(i, carry):
            up_sample(l, i)
            return carry
        lax.fori_loop(0, own, up_body, 0)
        for i in range(own):
            wait_like(xbuf.at[own + i], rx.at[i])
        lax.fori_loop(own, 2 * own, up_body, 0)
        advance(l, t_up, t_down)
        for i in range(own):
            part_sample(l, i, trans_part)
        sends_done(xbuf, sx)
        for i in range(own):
            resid_sample(l, 1, i, trans_part)
        sends_done(sbuf, sp)
        return carry

    lax.fori_loop(0, g.layers, layer, 0)

    PR = OUT_ROWS
    pieces = [(s, h) for s in range(own) for h in range(T // PR)]
    tpp, tpm, tpo = (v * CORES + c for v in (xp, xm, xo))

    def orow(blk, p, lo=0, n=PR):
        s, h = pieces[p]
        return out.at[blk * own + s, pl.ds(h * PR + lo, n)]

    def opush(r, dev, sem):
        remote(r, r, osend, sem, dev).start()

    def oawait(halves, sem):
        wait_like(out.at[0, pl.ds(0, halves * PR // 2)], sem)

    for p in range(len(pieces)):
        opush(orow(tp, p), dev_p, o_a.at[p])
        opush(orow(tp, p), dev_m, o_a.at[p])
        opush(orow(tp, p), dev_c, o_p0.at[p])
    for p in range(len(pieces)):
        oawait(4, o_a.at[p])
        opush(orow(tpm, p, 0, PR // 2), dev_p, o_d.at[p])
        opush(orow(tpp, p, PR // 2, PR // 2), dev_m, o_d.at[p])
        opush(orow(tpm, p), dev_c, o_p1.at[p])
        opush(orow(tpp, p), dev_c, o_p1.at[p])
    for p in range(len(pieces)):
        oawait(2, o_d.at[p])
        opush(orow(tpo, p), dev_c, o_p2.at[p])
    for p in range(len(pieces)):
        oawait(2, o_p0.at[p])
        oawait(4, o_p1.at[p])
        oawait(2, o_p2.at[p])
    wait_like(out.at[pl.ds(0, 7 * own)], osend)
    wait_like(buf.at[pl.ds(0, 3)], send)
    wait_like(bqbuf.at[pl.ds(0, nx - 1)], s_bq)


def finish(src, dst, sem):
    cp = pltpu.make_async_copy(src, dst, sem)
    cp.start()
    cp.wait()


def solution(mesh):
    def body(token_act, token_cond, pair_bias, token_mask, ada_scale, ada_w, ada_bias, zero_w, zero_b, w_qkvg, b_q, w_o, w_up, w_down):
        g = Geometry(mesh, token_act.shape, token_cond.shape, pair_bias.shape, w_qkvg.shape, w_up.shape)
        L, D, C, T, own, nx = g.layers, g.width, g.cond_dim, g.tokens, g.own, g.nx
        ada = ada_w.transpose(0, 1, 3, 2, 4).reshape(2 * L, 2, C, D)
        zero = zero_w.transpose(0, 2, 1, 3).reshape(2 * L, C, D)
        bq = jnp.pad(b_q, ((0, 8 - L), (0, LANES - g.lw)))
        vm = pl.BlockSpec(memory_space=pltpu.VMEM)
        hbm = pl.BlockSpec(memory_space=pl.ANY)
        dma = pltpu.SemaphoreType.DMA
        npc = own * (T // OUT_ROWS)
        K = g.chunks
        gathered = pl.pallas_call(
            functools.partial(kernel, g),
            out_shape=pltpu.VMEM(token_act.shape, BF16),
            in_specs=[hbm, hbm, hbm, vm, vm, hbm, vm, hbm, vm, hbm, hbm, hbm, hbm, hbm],
            out_specs=vm,
            scratch_shapes=[
                pltpu.VMEM((nx, g.rows, LANES), BF16),
                pltpu.VMEM((2 * own, T, D), BF16),
                pltpu.VMEM((own, T, D), BF16),
                pltpu.VMEM((own, T, D), BF16),
                pltpu.VMEM((2 * own, nx, T, LANES), BF16),
                pltpu.VMEM((2 * own, T, nx * g.hu), BF16),
                pltpu.VMEM((own, T, C), BF16),
                pltpu.VMEM((own, T, C), F32),
                pltpu.VMEM((2 * L, 2, C, D), BF16),
                pltpu.VMEM((2 * L, C, D), BF16),
                pltpu.VMEM((nx, 8, LANES), F32),
                pltpu.VMEM((g.heads, T, T), F32),
                pltpu.VMEM((T, LANES), BF16),
                pltpu.VMEM((T, LANES), BF16),
                pltpu.VMEM((T, LANES), BF16),
                pltpu.VMEM((T, LANES), F32),
                dma((L,)), dma((3,)), dma((2,)), dma,
                dma((K,)), dma((K,)), dma((K,)), dma((K,)),
                dma, dma, dma((own,)), dma((own,)), dma((own,)), dma((own,)),
                dma, dma((npc,)), dma((npc,)), dma((npc,)), dma((npc,)), dma((npc,)),
            ],
            compiler_params=pltpu.CompilerParams(collective_id=0, has_side_effects=True, vmem_limit_bytes=50 << 20),
            name='blocks',
        )(token_act, token_cond, pair_bias, token_mask.reshape(1, T), ada_scale.reshape(2 * L, 1, C), ada, ada_bias.reshape(2 * L, 1, D),
          zero, zero_b.reshape(2 * L, 1, D), w_qkvg.transpose(0, 2, 3, 1), bq, w_o, w_up.transpose(0, 2, 3, 1), w_down)
        gathered = pltpu.with_memory_space_constraint(gathered, pltpu.VMEM)
        return pl.pallas_call(
            finish,
            out_shape=jax.ShapeDtypeStruct(token_act.shape, BF16),
            in_specs=[vm],
            out_specs=pl.BlockSpec(memory_space=pltpu.HBM),
            scratch_shapes=[dma],
            compiler_params=pltpu.CompilerParams(vmem_limit_bytes=1 << 20),
            name='finish',
        )(gathered)

    everywhere = P()
    in_specs = (P('dp', None, None), P('dp', None, None), P(None, 'tp', None, None), P(None), everywhere, everywhere, everywhere, everywhere, everywhere, P(None, None, None, 'tp'), P(None, 'tp'), P(None, 'tp', None), P(None, None, None, 'tp'), P(None, 'tp', None))
    return jax.shard_map(body, mesh=mesh, in_specs=in_specs, out_specs=P('dp', None, None), check_vma=False)
```

time: 1150 us -> 268 us (0.23)
  matrix products: 457 us -> 0 us
  waiting for transfers between devices: 412 us -> 0 us
  Pallas kernels: 0 us -> 256 us
  other arithmetic: 202 us -> 0 us
  local copies, waits for them, and re-layouts: 56.6 us -> 11.6 us
  between operations: 13.9 us -> 0.01 us
    psum x4 -> x0, waiting for transfers between devices: 412 us -> none  [the longest x2 225 us: shard_body(): trans_out = lax.psum(trans_part, 'tp').astype(jnp.float32)]
    dot_general x42 -> x0, matrix products: 296 us -> none  [the longest x32 101 us: attend_sample(): jnp.einsum('hqk,khc->qhc', attn_probs, value_one, preferred_element_type=...]
    pallas_call x0 -> x2, Pallas kernels: none -> 256 us  [the longest x1 251 us: body(): pl.pallas_call(functools.partial(kernel, g), out_shape=pltpu.VMEM(token_a...]
    reduce_sum x10 -> x0, other arithmetic: 112 us -> none  [the longest x5 76.4 us: layer_norm(): row_mean = jnp.mean(values_in, axis=-1, keepdims=True)]
    unnamed x4 -> x0, matrix products: 89.1 us -> none
    sub x32 -> x0, matrix products: 71.7 us -> none  [attend_sample(): attn_probs = jax.nn.softmax(logits, axis=-1).astype(jnp.bfloat16)]
    convert_element_type x7 -> x0, other arithmetic: 68 us -> none  [the longest x1 24.8 us: ada_norm(): (jax.nn.sigmoid(modulation[:, 0] + bias_vec) * layer_norm(act_f32) + modu...]
    unnamed x80 -> x2, local copies, waits for them, and re-layouts: 25.5 us -> 0.01 us
  transfers between devices with their start and end apart: 4 -> 0, of which waited for: 4 -> 0; matrix products, arithmetic and copies ran while one was open for 12% -> 0% of each run, Pallas kernels for 0% -> 0%
where the time goes in v2:
time: 268 us; the launch traced here: 267 us
  Pallas kernels  256 us (96%)
  local copies, waits for them, and re-layouts  11.6 us (4%)
    pallas_call x1, Pallas kernels, body(): pl.pallas_call(functools.partial(kernel, g), out_shape=pltpu.VMEM(token_a...  251 us

profile of v2, /device:TPU:81, one launch (start us, length us, event | category | flops | bytes accessed | tf_op | source)
XLA Modules:
  0.0 267.3 jit_solution(11883625411395132853)
XLA Ops:
  0.0 1.3 pad.4.bq_in
  1.3 1.3 reshape.19.ascale_in
  2.6 1.3 reshape.21.abias_in
  3.9 1.3 reshape.23.zbias_in
  5.2 0.0 copy-start
  5.2 3.5 %copy.16 = bf16[2,2,384,768]{3,2,1,0:T(8,128)(2,1)} copy(bf16[2,2,384,768]{3,1,2,0:T(2,128)(2,1)} %bitcast.10) | data formatting | bytes 4718592 | tf_op jit(solution)/shard_map/transpose | solution.py:447
  8.7 0.0 copy-done
  8.7 2.8 %copy.15 = bf16[2,2,2,384,768]{4,3,2,1,0:T(8,128)(2,1)} copy(bf16[2,2,2,384,768]{4,2,3,1,0:T(2,128)(2,1)S(1)} %bitcast.9) | data formatting | bytes 9437184 | tf_op jit(solution)/shard_map/transpose | solution.py:446
  11.6 251.0 %blocks.1.src = bf16[16,512,768]{2,1,0:T(8,128)(2,1)S(1)} custom-call(bf16[16,512,768]{2,1,0:T(8,128)(2,1)} %act_in.1, bf16[16,512,384]{2,1,0:T(8,128)(2,1)} %cond_in.1, bf16[2,2,512,512]{3,2,1,0:T(8,128)(2,1)} %bias_in.1, s32[1,512]{1,0:T(1,128)} %bitcast.13, f32[4,1,384]{2,1,0:T(1,128)} %reshape.19.ascale_in, bf16[4,2,384,768]{3,2,1,0:T(8,128)(2,1)} %bitcast.7, ...), custom_call_target="tpu_custom_call" | custom-call | tf_op jit(solution)/shard_map/blocks/pallas_call | solution.py:454
  262.6 4.8 %finish.1 = bf16[16,512,768]{2,1,0:T(8,128)(2,1)} custom-call(bf16[16,512,768]{2,1,0:T(8,128)(2,1)S(1)} %blocks.1.src), custom_call_target="tpu_custom_call" | custom-call | tf_op jit(solution)/shard_map/finish/pallas_call | solution.py:486
Async XLA Ops:
  5.2 3.5 %copy-start = (bf16[2,2,384,2,768]{4,3,2,1,0:T(2,128)(2,1)S(1)}, bf16[2,2,384,2,768]{4,3,2,1,0:T(2,128)(2,1)}, u32[]{:S(2)}) copy-start(bf16[2,2,384,2,768]{4,3,2,1,0:T(2,128)(2,1)} %param.19) | copy-start | bytes 14155780

commit v3 on v2

v3 whole, which is shorter than its diff:
```python
import functools
import math
import jax
import jax.numpy as jnp
from jax import lax
from jax.experimental import pallas as pl
from jax.experimental.pallas import tpu as pltpu
from jax.sharding import PartitionSpec as P

LN_EPS = 1e-5
LOG2E = 1.4426950408889634
MESH = pl.DeviceIdType.MESH
BF16 = jnp.bfloat16
F32 = jnp.float32
LANES = 128
CH = 1056
LA = 4
TAIL_TICKS = 7
RELAY_AT = 2
HELD = 2
LAGS = (0, 1, 2)
RB = 512
OUT_ROWS = 256
CORES = 2


def dot_nt(lhs, rhs):
    return lax.dot_general(lhs, rhs, (((1,), (1,)), ((), ())), preferred_element_type=F32)


def dot_nn(lhs, rhs):
    return lax.dot_general(lhs, rhs, (((1,), (0,)), ((), ())), preferred_element_type=F32)


def normed(values_in):
    row_mean = jnp.mean(values_in, axis=-1, keepdims=True)
    centered = values_in - row_mean
    variance = jnp.mean(centered * centered, axis=-1, keepdims=True)
    return centered * lax.rsqrt(variance + LN_EPS)


class Geometry:
    def __init__(self, mesh, act, cond, bias, w_qkvg, w_up):
        self.nx = mesh.shape['tp'] // CORES
        self.y_stride = len({d.coords[2] for d in mesh.devices.flat})
        self.samples, self.tokens, self.width = act
        self.cond_dim = cond[-1]
        self.layers, self.heads = bias[0], bias[1]
        self.lw = w_qkvg[-1]
        self.hd = self.lw // self.heads
        self.hu = w_up[-1]
        self.own = self.samples // mesh.shape['tp']
        self.ncol = self.width // LANES
        self.tcol = self.tokens // LANES
        self.q0 = 0
        self.b0 = self.q0 + self.ncol * 4 * self.lw
        self.o0 = self.b0 + self.heads * self.tcol * self.tokens
        self.u0 = self.o0 + self.ncol * self.lw
        self.d0 = self.u0 + self.ncol * 2 * self.hu
        self.lr = self.d0 + self.ncol * self.hu
        self.flat_rows = self.layers * self.lr - self.o0
        self.chunks = -(-self.flat_rows // CH)
        self.rows = self.chunks * CH
        assert self.lw == 96 and self.hu == 192 and self.heads == 2 and self.nx == 4 and self.layers == 2 and self.own == 2


def kernel(g, act_in, cond_in, bias_in, mask_in, ascale_in, ada_in, abias_in, zero_in, zbias_in, wq_in, bq_in, wo_in, up_in, down_in,
           out, buf, qb0, xbuf, abuf, pbuf, obuf, hbuf, cring, cbuf, lnbuf, adabuf, zerobuf, bqbuf, bmbuf, qa, ka, va, ga, qb, kb, vb, gb,
           s_loc, s_act, s_ada, s_in, send, ra, rb, rc, rd, s_bq, r_bq, sx0, rx0, s_o, r_o, r_rel, sx, rx, sp, rp, osend, o_p0, o_a, o_p1, o_d, o_p2):
    nx, own, T, D = g.nx, g.own, g.tokens, g.width
    lw, hu, hd = g.lw, g.hu, g.hd
    half = hu - LANES
    tp = lax.axis_index('tp')
    dp = lax.axis_index('dp')
    x = tp // CORES
    c = lax.rem(tp, CORES)
    xp = lax.rem(x + 1, nx)
    xm = lax.rem(x + nx - 1, nx)
    xo = lax.rem(x + 2, nx)
    dev_p, dev_m, dev_o = ({'tp': v * CORES + c} for v in (xp, xm, xo))
    dev_c = {'tp': x * CORES + 1 - c}
    pz = lax.rem(dp, 2)
    py = lax.rem(dp // g.y_stride, 2)
    dev_z = {'dp': dp + 1 - 2 * pz}
    dev_y = {'dp': dp + g.y_stride * (1 - 2 * py)}
    mine = tp * own

    def remote(src, dst, s_sem, r_sem, dev):
        return pltpu.make_async_remote_copy(src, dst, s_sem, r_sem, device_id=dev, device_id_type=MESH)

    def wait_like(ref, sem):
        pltpu.make_async_copy(ref, ref, sem).wait()

    barrier = pltpu.get_barrier_semaphore()
    devs = (dev_p, dev_m, dev_o, dev_c, dev_z, dev_y)
    for d in devs:
        pl.semaphore_signal(barrier, inc=1, device_id=d, device_id_type=MESH)

    steps = nx * own

    def chip_of(n):
        near = jnp.where(lax.rem(n, 2) == 0, 1, nx - 1)
        return lax.rem(x + jnp.where(n < own, 2, jnp.where(n < 3 * own, near, 0)), nx)

    def pair_of(n):
        return jnp.where((n < own) | (n >= 3 * own), lax.rem(n, own), (n - own) // 2)

    def sample_of(n, core):
        return chip_of(n) * (CORES * own) + pair_of(n) * CORES + core

    def load_sample(n):
        slot = lax.rem(n, 2 * own)
        pltpu.make_async_copy(act_in.at[sample_of(n, c)], hbuf.at[slot], s_in.at[0, slot]).start()
        pltpu.make_async_copy(cond_in.at[sample_of(n, c)], cring.at[slot], s_in.at[1, slot]).start()

    load_sample(0)
    ada_cps = [pltpu.make_async_copy(ada_in.at[v], adabuf.at[v], s_ada.at[v]) for v in range(2 * g.layers)]
    zero_cps = [pltpu.make_async_copy(zero_in.at[v], zerobuf.at[v], s_ada.at[2 * g.layers + v]) for v in range(2 * g.layers)]
    ada_cps[0].start()

    q_parts = ((0, 0, lw, 0), (3, 0, 32, lw), (1, 0, lw, LANES), (3, 32, 32, LANES + lw), (2, 0, lw, 2 * LANES), (3, 64, 32, 2 * LANES + lw))
    u_parts = ((0, 0, LANES, 0), (0, LANES, half, LANES), (1, LANES, half, LANES + half), (1, 0, LANES, 2 * LANES))

    def load_attn(l, place, sem):
        for j in range(g.ncol):
            for f, r0, n, off in q_parts:
                pltpu.make_async_copy(wq_in.at[l, f, pl.ds(r0, n), pl.ds(j * LANES, LANES)], place(g.q0 + j * 4 * lw + off, n), sem).start()
        for h in range(g.heads):
            for j in range(g.tcol):
                pltpu.make_async_copy(bias_in.at[l, h, :, pl.ds(j * LANES, LANES)], place(g.b0 + (h * g.tcol + j) * T, T), sem).start()

    def load_rest(l, place, sem):
        for j in range(g.ncol):
            col = pl.ds(j * LANES, LANES)
            pltpu.make_async_copy(wo_in.at[l, :, col], place(g.o0 + j * lw, lw), sem).start()
            for f, r0, n, off in u_parts:
                pltpu.make_async_copy(up_in.at[l, f, pl.ds(r0, n), col], place(g.u0 + j * 2 * hu + off, n), sem).start()
            pltpu.make_async_copy(down_in.at[l, :, col], place(g.d0 + j * hu, hu), sem).start()

    def own_rows(l):
        return lambda off, n: buf.at[x, pl.ds(l * g.lr - g.o0 + off, n)]

    load_rest(0, own_rows(0), s_loc.at[1])
    act_cp = pltpu.make_async_copy(act_in.at[pl.ds(mine, own)], abuf, s_act.at[0])
    cond_cp = pltpu.make_async_copy(cond_in.at[pl.ds(mine, own)], cbuf, s_act.at[1])
    bqbuf[x] = jnp.zeros((8, LANES), F32)
    bqbuf[x, pl.ds(0, g.layers), pl.ds(0, lw)] = bq_in[...]

    pad = g.rows - g.flat_rows
    if pad:
        buf[x, pl.ds(g.flat_rows, pad), :] = jnp.zeros((pad, LANES), BF16)

    Q = CH // 4
    g0 = 2 * py + pz
    gy = 2 * (1 - py) + pz
    gz = 2 * py + 1 - pz
    gd = 2 * (1 - py) + 1 - pz

    def push(blk, k, part, dev, r_sem):
        r = buf.at[blk, pl.ds(pl.multiple_of(k * CH + part * Q, 8), Q)]
        remote(r, r, send, r_sem, dev).start()

    def await_quarters(n, sem):
        wait_like(buf.at[0, pl.ds(0, n * Q)], sem)

    def first(k):
        push(x, k, g0, dev_p, ra.at[k])
        push(x, k, g0, dev_m, ra.at[k])

    def stage1(k):
        await_quarters(2, ra.at[k])
        push(xm, k, g0, dev_p, rd.at[k])
        for blk in (xm, xp):
            push(blk, k, g0, dev_y, rb.at[k])
            push(blk, k, g0, dev_z, rb.at[k])

    def stage2(k):
        await_quarters(4, rb.at[k])
        push(xm, k, gy, dev_p, rd.at[k])
        push(xp, k, gz, dev_m, rd.at[k])
        push(xm, k, gz, dev_y, rc.at[k])
        push(xp, k, gy, dev_z, rc.at[k])

    def stage3(k):
        await_quarters(2, rc.at[k])
        push(xp, k, gd, dev_m, rd.at[k])

    def stage4(k):
        await_quarters(4, rd.at[k])

    K = g.chunks

    def tick(t):
        @pl.when(t + LA < K)
        def _():
            first(t + LA)
        for lag, stage in zip(LAGS, (stage1, stage2, stage3)):
            @pl.when((t >= lag) & (t - lag < K))
            def _(lag=lag, stage=stage):
                stage(t - lag)

    def need(rows_end, lag):
        return -(-(rows_end - g.o0) // CH) + lag

    lane = lax.broadcasted_iota(jnp.int32, (1, LANES), 1)
    mask_add = (mask_in[...].astype(F32) - 1.0) * (1e9 * LOG2E)
    scale2 = LOG2E / math.sqrt(hd)

    def modulated(l, j, cond_ln, act_f32):
        c_in = (cond_ln * ascale_in[l, pl.ds(j, 1), :]).astype(BF16)
        gain = jax.nn.sigmoid(dot_nn(c_in, adabuf[l * 2 + j, 0]) + abias_in[l, pl.ds(j, 1), :])
        shift = dot_nn(c_in, adabuf[l * 2 + j, 1])
        return (gain * normed(act_f32) + shift).astype(BF16)

    def row_blocks(body):
        for r in range(T // RB):
            body(pl.ds(r * RB, RB))

    def ada_sample(l, j, i):
        def rows_body(rows):
            xbuf[i, rows, :] = modulated(l, j, lnbuf[i, rows, :], abuf[i, rows, :].astype(F32))
        row_blocks(rows_body)
        remote(xbuf.at[i], xbuf.at[own + i], sx.at[i], rx.at[i], dev_c).start()

    stage0 = 2 * own * nx

    def relay_box(v):
        return xbuf.at[v, :, pl.ds(0, LANES)]

    def sent_part(i):
        return obuf.at[pl.ds(stage0 + i * g.ncol, g.ncol)]

    def got_part(i):
        return pbuf.at[pl.ds(i * g.ncol, g.ncol)]

    def resid_sample(l, j, i, part_of):
        rows = pl.ds(0, T)
        ours = part_of(l, i, rows)
        gate = jax.nn.sigmoid(dot_nn(cbuf[i], zerobuf[l * 2 + j]) + zbias_in[l, pl.ds(j, 1), :])
        wait_like(got_part(i), rp.at[i])
        theirs = jnp.concatenate([pbuf[i * g.ncol + v] for v in range(g.ncol)], axis=1)
        act = (abuf[i].astype(F32) + gate * (ours + theirs.astype(F32)).astype(BF16).astype(F32)).astype(BF16)
        abuf[i] = act
        if j == 1:
            out[mine + i] = act

    def part_sample(l, i, part_of):
        def rows_body(rows):
            part = part_of(l, own + i, rows).astype(BF16)
            for v in range(g.ncol):
                obuf[stage0 + i * g.ncol + v, rows, :] = part[:, v * LANES:(v + 1) * LANES]
        row_blocks(rows_body)
        remote(sent_part(i), got_part(i), sp.at[i], rp.at[i], dev_c).start()

    def flat(s, l, off, n):
        return buf[s, pl.ds(pl.multiple_of(l * g.lr - g.o0 + off, 8), n), :]

    def bias_prep(rows_of):
        for h in range(g.heads):
            for j in range(g.tcol):
                col = pl.ds(j * LANES, LANES)
                bmbuf[h, :, col] = rows_of(g.b0 + (h * g.tcol + j) * T, T).astype(F32) * LOG2E + mask_add[:, j * LANES:(j + 1) * LANES]

    def project(slot, x_rows, rows_of, q_bias):
        qs, ks, vs, gs = slot
        w = jnp.concatenate([rows_of(g.q0 + j * 4 * lw, 4 * lw) for j in range(g.ncol)], axis=1)
        proj = dot_nt(x_rows, w)
        pa, pb, pc = (proj[:, v * LANES:(v + 1) * LANES] for v in range(3))
        qs[...] = (pa + q_bias).astype(BF16)
        ks[...] = pb.astype(BF16)
        vs[...] = jnp.where(lane < lw, pc, 1.0).astype(BF16)
        gate = jnp.where(lane < 32, pltpu.roll(pa, 32, 1), jnp.where(lane < 64, pltpu.roll(pb, 64, 1), pltpu.roll(pc, 96, 1)))
        gs[...] = jnp.where(lane < lw, jax.nn.sigmoid(gate), 0.0)

    def attend(slot, o_ref):
        qs, ks, vs, gs = slot
        q = qs[...]
        zero = jnp.zeros((), BF16)
        both = jnp.concatenate([jnp.where((lane >= h * hd) & (lane < (h + 1) * hd), q, zero) for h in range(g.heads)], axis=0)
        z = dot_nt(both, ks[...]) * scale2 + jnp.concatenate([bmbuf[h] for h in range(g.heads)], axis=0)
        e = jnp.exp2(z - jnp.max(z, axis=-1, keepdims=True)).astype(BF16)
        o = dot_nn(e, vs[...])
        o = o * (1.0 / o[:, lw:lw + 1])
        o_ref[...] = (jnp.where(lane < hd, o[:T], o[T:]) * gs[...]).astype(BF16)

    slot_a = (qa, ka, va, ga)
    slot_b = (qb, kb, vb, gb)

    def ada_first(n):
        slot = lax.rem(n, 2 * own)
        s = sample_of(n, c)
        wait_like(hbuf.at[slot], s_in.at[0, slot])
        wait_like(cring.at[slot], s_in.at[1, slot])
        def rows_body(rows):
            out[s, rows, :] = modulated(0, 0, normed(cring[slot, rows, :].astype(F32)), hbuf[slot, rows, :].astype(F32))
        row_blocks(rows_body)
        remote(out.at[s], out.at[s], sx0, rx0.at[n], dev_c).start()
        @pl.when(n + 2 * own < steps)
        def _():
            load_sample(n + 2 * own)

    def qb_rows(off, n):
        return qb0[pl.ds(off, n), :]

    ada_cps[0].wait()
    load_attn(0, lambda off, n: qb0.at[pl.ds(off, n)], s_loc.at[0])
    for n in range(1, 2 * own):
        load_sample(n)
    load_attn(1, own_rows(1), s_loc.at[2])
    load_rest(1, own_rows(1), s_loc.at[2])
    for cp in (cond_cp, act_cp, zero_cps[0], *ada_cps[1:], *zero_cps[1:]):
        cp.start()
    pl.semaphore_wait(barrier, len(devs))
    wait_like(buf.at[x, pl.ds(0, g.lr - g.o0)], s_loc.at[1])
    early = (g.lr - g.o0) // CH
    for k in range(min(LA, early)):
        first(k)
    ada_first(0)
    wait_like(qb0, s_loc.at[0])
    bias_prep(qb_rows)
    for d in (dev_p, dev_m, dev_o):
        remote(bqbuf.at[x], bqbuf.at[x], s_bq, r_bq, d).start()
    q_bias0 = bqbuf[x, pl.ds(0, 1), :]
    project(slot_a, out[sample_of(0, c)], qb_rows, q_bias0)
    wait_like(buf.at[x, pl.ds(0, g.lr)], s_loc.at[2])
    for k in range(min(LA, early), LA):
        first(k)

    def first_steps(m, carry):
        @pl.when(m + 1 < steps)
        def _():
            ada_first(m + 1)

        def slot_of(pair, core):
            return jnp.where(pair == c, 0, own) + core

        def place_of(u, core):
            slot = slot_of(pair_of(m), core) * nx + x
            return slot, jnp.where(m < steps - own, stage0 + CORES * m + u, slot)

        def send(u, slot, place):
            @pl.when(m == 0)
            def _():
                remote(obuf.at[place], relay_box(u), s_o, r_rel.at[u], dev_p).start()

            @pl.when(m == 1)
            def _():
                remote(obuf.at[place], relay_box(CORES + u), s_o, r_rel.at[CORES + u], dev_m).start()

            @pl.when((m >= own) & (m < steps - own))
            def _():
                remote(obuf.at[place], obuf.at[slot], s_o, r_o, {'tp': chip_of(m) * CORES + c}).start()

        def forward(pair, dev, source):
            for u, core in enumerate((c, 1 - c)):
                r = relay_box(pair * CORES + u)
                wait_like(r, r_rel.at[pair * CORES + u])
                remote(r, obuf.at[slot_of(pair, core) * nx + source], s_o, r_o, dev).start()

        @pl.when(m == own)
        def _():
            forward(0, dev_p, xm)

        @pl.when(m == own + 1)
        def _():
            forward(1, dev_m, xp)
        wait_like(out.at[0], rx0.at[m])
        slot, place = place_of(0, c)
        attend(slot_a, obuf.at[place])
        project(slot_b, out[sample_of(m, 1 - c)], qb_rows, q_bias0)
        send(0, slot, place)
        slot, place = place_of(1, 1 - c)
        attend(slot_b, obuf.at[place])
        project(slot_a, out[sample_of(jnp.minimum(m + 1, steps - 1), c)], qb_rows, q_bias0)
        send(1, slot, place)

        @pl.when(m >= HELD)
        def _():
            tick(m - HELD)
        return carry
    lax.fori_loop(0, steps, first_steps, 0)

    cond_cp.wait()
    act_cp.wait()
    for i in range(own):
        lnbuf[i] = normed(cbuf[i].astype(F32))
    for cp in (*ada_cps[1:], *zero_cps):
        cp.wait()
    remote_pieces = CORES * (steps - own)
    wait_like(obuf.at[pl.ds(stage0, remote_pieces)], r_o)
    wait_like(obuf.at[pl.ds(0, remote_pieces + CORES * own)], s_o)
    wait_like(out.at[pl.ds(0, steps)], sx0)

    def attn_part(l, i, rows):
        lhs = jnp.concatenate([obuf[i * nx + s, rows, :] for s in range(nx)], axis=1)
        zpad = jnp.zeros((LANES - lw, LANES), BF16)
        rhs = jnp.concatenate([jnp.concatenate([v for s in range(nx) for v in (flat(s, l, g.o0 + j * lw, lw), zpad)], axis=0) for j in range(g.ncol)], axis=1)
        return dot_nn(lhs, rhs)

    def up_sample(l, i):
        y = xbuf[i]
        for p in range(nx // 2):
            w = jnp.concatenate([jnp.concatenate([flat(2 * p + e, l, g.u0 + j * 2 * hu, 2 * hu) for j in range(g.ncol)], axis=1) for e in range(2)], axis=0)
            u = dot_nt(y, w)
            mids = []
            for e in range(2):
                ua, ub, uc = (u[:, (3 * e + v) * LANES:(3 * e + v + 1) * LANES] for v in range(3))
                side = (3 * p + 2 * e) * LANES
                hbuf[i, :, side:side + LANES] = (jax.nn.silu(ua) * uc).astype(BF16)
                act = jax.nn.silu(ub)
                mids.append(act * pltpu.roll(ub, half, 1) if e == 0 else pltpu.roll(act, half, 1) * ub)
            mid = (3 * p + 1) * LANES
            hbuf[i, :, mid:mid + LANES] = jnp.where(lane < half, mids[0], mids[1]).astype(BF16)

    def trans_part(l, i, rows):
        cols = []
        for j in range(g.ncol):
            v = []
            for p in range(nx // 2):
                v.append(flat(2 * p, l, g.d0 + j * hu, hu))
                v.append(flat(2 * p + 1, l, g.d0 + j * hu + LANES, half))
                v.append(flat(2 * p + 1, l, g.d0 + j * hu, LANES))
            cols.append(jnp.concatenate(v, axis=0))
        return dot_nn(hbuf[i, rows, :], jnp.concatenate(cols, axis=1))

    PR = OUT_ROWS
    npc = T // PR
    tpp, tpm, tpo = (v * CORES + c for v in (xp, xm, xo))

    def orow(blk, p, lo=0, n=PR):
        return out.at[blk * own + p // npc, pl.ds(pl.multiple_of(lax.rem(p, npc) * PR, PR) + lo, n)]

    def opush(r, dev, sem):
        remote(r, r, osend, sem, dev).start()

    def oawait(halves, sem):
        wait_like(out.at[0, pl.ds(0, halves * PR // 2)], sem)

    def out_first(i):
        for h in range(npc):
            p = i * npc + h
            opush(orow(tp, p), dev_p, o_a.at[p])
            opush(orow(tp, p), dev_m, o_a.at[p])
            opush(orow(tp, p), dev_c, o_p0.at[p])

    def out_relay(p):
        oawait(4, o_a.at[p])
        opush(orow(tpm, p, 0, PR // 2), dev_p, o_d.at[p])
        opush(orow(tpp, p, PR // 2, PR // 2), dev_m, o_d.at[p])
        opush(orow(tpm, p), dev_c, o_p1.at[p])
        opush(orow(tpp, p), dev_c, o_p1.at[p])

    t0 = steps - HELD
    t1 = t0 + TAIL_TICKS
    assert K + LAGS[-1] <= t1 + nx * own and need(g.lr, LAGS[-1]) <= t0 + 4

    def arrived(lo, hi):
        for k in range(lo, hi):
            stage4(k)

    k_o, k_u, k_d = (need(v, 0) for v in (g.u0, g.d0, g.lr))
    def each(count):
        def run(body):
            def step(i, carry):
                body(i)
                return carry
            lax.fori_loop(0, count, step, 0)
        return run

    arrived(0, k_o)

    @each(own)
    def _(i):
        part_sample(0, i, attn_part)
    tick(t0)

    @each(own)
    def _(i):
        resid_sample(0, 0, i, attn_part)
        ada_sample(0, 1, i)
        tick(t0 + 1 + i)
    arrived(k_o, k_u)

    @each(2 * own)
    def _(i):
        @pl.when(i >= own)
        def _():
            wait_like(xbuf.at[0], rx.at[i - own])
        up_sample(0, i)

        @pl.when(lax.rem(i, 2) == 1)
        def _():
            tick(t0 + 3 + i // 2)
    arrived(k_u, k_d)

    @each(own)
    def _(i):
        wait_like(sent_part(0), sp.at[i])
        part_sample(0, i, trans_part)
        wait_like(xbuf.at[0], sx.at[i])

    @each(own)
    def _(i):
        resid_sample(0, 1, i, trans_part)
        ada_sample(1, 0, i)
        tick(t0 + 5 + i)
    wait_like(bqbuf.at[pl.ds(0, nx - 1)], r_bq)

    k_q, k_o, k_u, k_d = (need(g.lr + v, 0) for v in (g.o0, g.u0, g.d0, g.lr))
    first_k = need(g.lr, 0)

    def shard_of(q):
        return lax.rem(x + jnp.where(q == 0, 0, jnp.where(q == 1, nx - 1, q - 1)), nx)

    def rows_from(s):
        return lambda off, n: flat(s, 1, off, n)

    def q_bias1(s):
        return bqbuf[s, pl.ds(1, 1), :]

    def half_layer(hf, carry):
        def once(body):
            pl.when(hf == 0)(body)

        project(slot_a, xbuf[hf], rows_from(x), q_bias1(x))
        wait_like(xbuf.at[own + hf], rx.at[hf])

        def shard(q, inner):
            s = shard_of(q)
            after = shard_of(jnp.minimum(q + 1, nx - 1))
            bias_prep(rows_from(s))
            pl.when((hf > 0) & (q == RELAY_AT))(lambda: out_relay(0))
            attend(slot_a, obuf.at[hf * nx + s])
            project(slot_b, xbuf[own + hf], rows_from(s), q_bias1(s))

            @pl.when(hf == 0)
            def _():
                tick(t1 + 2 * q)

                @pl.when(q == nx - 2)
                def _():
                    arrived(first_k, k_q)
            attend(slot_b, obuf.at[(own + hf) * nx + s])
            project(slot_a, xbuf[hf], rows_from(after), q_bias1(after))
            once(lambda: tick(t1 + 2 * q + 1))
            return inner
        lax.fori_loop(0, nx, shard, 0)
        once(lambda: arrived(k_q, k_o))
        wait_like(sent_part(hf), sp.at[hf])
        part_sample(1, hf, attn_part)
        wait_like(xbuf.at[hf], sx.at[hf])
        resid_sample(1, 0, hf, attn_part)
        ada_sample(1, 1, hf)
        once(lambda: arrived(k_o, k_u))
        pl.when(hf > 0)(lambda: out_relay(1))
        up_sample(1, hf)
        wait_like(xbuf.at[own + hf], rx.at[hf])
        up_sample(1, own + hf)
        once(lambda: arrived(k_u, k_d))
        wait_like(sent_part(hf), sp.at[hf])
        part_sample(1, hf, trans_part)
        resid_sample(1, 1, hf, trans_part)
        out_first(hf)
        return carry

    lax.fori_loop(0, own, half_layer, 0)
    for i in range(own):
        wait_like(xbuf.at[i], sx.at[i])
        wait_like(sent_part(i), sp.at[i])
    for p in range(npc, own * npc):
        out_relay(p)
    for p in range(own * npc):
        oawait(2, o_d.at[p])
        opush(orow(tpo, p), dev_c, o_p2.at[p])
    for p in range(own * npc):
        oawait(2, o_p0.at[p])
        oawait(4, o_p1.at[p])
        oawait(2, o_p2.at[p])
    wait_like(out.at[pl.ds(0, 7 * own)], osend)
    wait_like(buf.at[pl.ds(0, 3)], send)
    wait_like(bqbuf.at[pl.ds(0, nx - 1)], s_bq)


def finish(src, dst, sem):
    cp = pltpu.make_async_copy(src, dst, sem)
    cp.start()
    cp.wait()


def solution(mesh):
    def body(token_act, token_cond, pair_bias, token_mask, ada_scale, ada_w, ada_bias, zero_w, zero_b, w_qkvg, b_q, w_o, w_up, w_down):
        g = Geometry(mesh, token_act.shape, token_cond.shape, pair_bias.shape, w_qkvg.shape, w_up.shape)
        L, D, C, T, own, nx = g.layers, g.width, g.cond_dim, g.tokens, g.own, g.nx
        ada = ada_w.transpose(0, 1, 3, 2, 4).reshape(2 * L, 2, C, D)
        zero = zero_w.transpose(0, 2, 1, 3).reshape(2 * L, C, D)
        vm = pl.BlockSpec(memory_space=pltpu.VMEM)
        hbm = pl.BlockSpec(memory_space=pl.ANY)
        dma = pltpu.SemaphoreType.DMA
        npc = own * (T // OUT_ROWS)
        K = g.chunks
        steps = nx * own
        gathered = pl.pallas_call(
            functools.partial(kernel, g),
            out_shape=pltpu.VMEM(token_act.shape, BF16),
            in_specs=[hbm, hbm, hbm, vm, vm, hbm, vm, hbm, vm, hbm, vm, hbm, hbm, hbm],
            out_specs=vm,
            scratch_shapes=[
                pltpu.VMEM((nx, g.rows, LANES), BF16),
                pltpu.VMEM((g.o0, LANES), BF16),
                pltpu.VMEM((2 * own, T, D), BF16),
                pltpu.VMEM((own, T, D), BF16),
                pltpu.VMEM((own * g.ncol, T, LANES), BF16),
                pltpu.VMEM((2 * own * nx + own * g.ncol, T, LANES), BF16),
                pltpu.VMEM((2 * own, T, nx * g.hu), BF16),
                pltpu.VMEM((2 * own, T, C), BF16),
                pltpu.VMEM((own, T, C), BF16),
                pltpu.VMEM((own, T, C), F32),
                pltpu.VMEM((2 * L, 2, C, D), BF16),
                pltpu.VMEM((2 * L, C, D), BF16),
                pltpu.VMEM((nx, 8, LANES), F32),
                pltpu.VMEM((g.heads, T, T), F32),
                pltpu.VMEM((T, LANES), BF16),
                pltpu.VMEM((T, LANES), BF16),
                pltpu.VMEM((T, LANES), BF16),
                pltpu.VMEM((T, LANES), F32),
                pltpu.VMEM((T, LANES), BF16),
                pltpu.VMEM((T, LANES), BF16),
                pltpu.VMEM((T, LANES), BF16),
                pltpu.VMEM((T, LANES), F32),
                dma((3,)), dma((3,)), dma((4 * L,)), dma((2, 2 * own)), dma,
                dma((K,)), dma((K,)), dma((K,)), dma((K,)),
                dma, dma, dma, dma((steps,)), dma, dma, dma((CORES * own,)),
                dma((own,)), dma((own,)), dma((own,)), dma((own,)),
                dma, dma((npc,)), dma((npc,)), dma((npc,)), dma((npc,)), dma((npc,)),
            ],
            compiler_params=pltpu.CompilerParams(collective_id=0, has_side_effects=True, vmem_limit_bytes=207 << 18),
            name='blocks',
        )(token_act, token_cond, pair_bias, token_mask.reshape(1, T), ada_scale, ada, ada_bias, zero, zero_b, w_qkvg.transpose(0, 2, 3, 1), b_q, w_o, w_up.transpose(0, 2, 3, 1), w_down)
        gathered = pltpu.with_memory_space_constraint(gathered, pltpu.VMEM)
        return pl.pallas_call(
            finish,
            out_shape=jax.ShapeDtypeStruct(token_act.shape, BF16),
            in_specs=[vm],
            out_specs=pl.BlockSpec(memory_space=pltpu.HBM),
            scratch_shapes=[dma],
            compiler_params=pltpu.CompilerParams(vmem_limit_bytes=1 << 20),
            name='finish',
        )(gathered)

    everywhere = P()
    in_specs = (P('dp', None, None), P('dp', None, None), P(None, 'tp', None, None), P(None), everywhere, everywhere, everywhere, everywhere, everywhere, P(None, None, None, 'tp'), P(None, 'tp'), P(None, 'tp', None), P(None, None, None, 'tp'), P(None, 'tp', None))
    return jax.shard_map(body, mesh=mesh, in_specs=in_specs, out_specs=P('dp', None, None), check_vma=False)
```

time: 268 us -> 190 us (0.71)
  Pallas kernels: 256 us -> 184 us
  local copies, waits for them, and re-layouts: 11.6 us -> 6.35 us
    pallas_call x1, Pallas kernels: 251 us -> 179 us  [body(): pl.pallas_call(functools.partial(kernel, g), out_shape=pltpu.VMEM(token_a...]
    reshape x3 -> x0, local copies, waits for them, and re-layouts: 3.95 us -> none  [the longest x1 1.33 us: body(): ada_bias.reshape(2 * L, 1, D)]
where the time goes in v3:
time: 190 us
  Pallas kernels  184 us (97%)
  local copies, waits for them, and re-layouts  6.35 us (3%)
    pallas_call x1, Pallas kernels, body(): pl.pallas_call(functools.partial(kernel, g), out_shape=pltpu.VMEM(token_a...  179 us
    pallas_call x1, Pallas kernels, body(): pl.pallas_call(finish, out_shape=jax.ShapeDtypeStruct(token_act.shape, BF...  4.79 us

profile of v3, /device:TPU:81, one launch (start us, length us, event | category | flops | bytes accessed | tf_op | source)
XLA Modules:
  0.0 190.3 jit_solution(15385053669870057231)
XLA Ops:
  0.0 0.0 copy-start
  0.0 3.5 %copy.16 = bf16[2,2,384,768]{3,2,1,0:T(8,128)(2,1)} copy(bf16[2,2,384,768]{3,1,2,0:T(2,128)(2,1)} %bitcast.10) | data formatting | bytes 4718592 | tf_op jit(solution)/shard_map/transpose | solution.py:595
  3.5 0.0 copy-done
  3.5 2.8 %copy.15 = bf16[2,2,2,384,768]{4,3,2,1,0:T(8,128)(2,1)} copy(bf16[2,2,2,384,768]{4,2,3,1,0:T(2,128)(2,1)S(1)} %bitcast.9) | data formatting | bytes 9437184 | tf_op jit(solution)/shard_map/transpose | solution.py:594
  6.3 178.9 %blocks.1.src = bf16[16,512,768]{2,1,0:T(8,128)(2,1)S(1)} custom-call(bf16[16,512,768]{2,1,0:T(8,128)(2,1)} %act_in.1, bf16[16,512,384]{2,1,0:T(8,128)(2,1)} %cond_in.1, bf16[2,2,512,512]{3,2,1,0:T(8,128)(2,1)} %bias_in.1, s32[1,512]{1,0:T(1,128)} %bitcast.13, f32[2,2,384]{2,1,0:T(2,128)} %ascale_in.1, bf16[4,2,384,768]{3,2,1,0:T(8,128)(2,1)} %bitcast.7, ...), custom_call_target="tpu_custom_call" | custom-call | tf_op jit(solution)/shard_map/blocks/pallas_call | solution.py:602
  185.3 4.8 %finish.1 = bf16[16,512,768]{2,1,0:T(8,128)(2,1)} custom-call(bf16[16,512,768]{2,1,0:T(8,128)(2,1)S(1)} %blocks.1.src), custom_call_target="tpu_custom_call" | custom-call | tf_op jit(solution)/shard_map/finish/pallas_call | solution.py:640
Async XLA Ops:
  0.0 3.5 %copy-start = (bf16[2,2,384,2,768]{4,3,2,1,0:T(2,128)(2,1)S(1)}, bf16[2,2,384,2,768]{4,3,2,1,0:T(2,128)(2,1)}, u32[]{:S(2)}) copy-start(bf16[2,2,384,2,768]{4,3,2,1,0:T(2,128)(2,1)} %param.19) | copy-start | bytes 14155780

commit v4 on v3

--- a/solution.py
+++ b/solution.py
@@ -13,12 +13,11 @@
 BF16 = jnp.bfloat16
 F32 = jnp.float32
 LANES = 128
-CH = 1056
+CH = 1216
 LA = 4
-TAIL_TICKS = 7
-RELAY_AT = 2
-HELD = 2
-LAGS = (0, 1, 2)
+TAIL_TICKS = 6
+HELD = 0
+LAGS = (0, 2, 5)
 RB = 512
 OUT_ROWS = 256
 CORES = 2
@@ -65,8 +64,8 @@
 
 
 def kernel(g, act_in, cond_in, bias_in, mask_in, ascale_in, ada_in, abias_in, zero_in, zbias_in, wq_in, bq_in, wo_in, up_in, down_in,
-           out, buf, qb0, xbuf, abuf, pbuf, obuf, hbuf, cring, cbuf, lnbuf, adabuf, zerobuf, bqbuf, bmbuf, qa, ka, va, ga, qb, kb, vb, gb,
-           s_loc, s_act, s_ada, s_in, send, ra, rb, rc, rd, s_bq, r_bq, sx0, rx0, s_o, r_o, r_rel, sx, rx, sp, rp, osend, o_p0, o_a, o_p1, o_d, o_p2):
+           out, buf, qb0, xbuf, abuf, pbuf, sbuf, obuf, hbuf, cring, cbuf, lnbuf, adabuf, zerobuf, bqbuf, mcol, bmbuf, qa, ka, va, ga, qb, kb, vb, gb,
+           s_loc, s_act, s_bias, s_ada, s_in, send, ra, rb, rc, rd, s_bq, r_bq, sx0, rx0, s_o, r_o, r_rel, sx, rx, sp, rp, osend, o_p0, o_a, o_p1, o_d, o_p2):
     nx, own, T, D = g.nx, g.own, g.tokens, g.width
     lw, hu, hd = g.lw, g.hu, g.hd
     half = hu - LANES
@@ -118,16 +117,23 @@
     zero_cps = [pltpu.make_async_copy(zero_in.at[v], zerobuf.at[v], s_ada.at[2 * g.layers + v]) for v in range(2 * g.layers)]
     ada_cps[0].start()
 
-    q_parts = ((0, 0, lw, 0), (3, 0, 32, lw), (1, 0, lw, LANES), (3, 32, 32, LANES + lw), (2, 0, lw, 2 * LANES), (3, 64, 32, 2 * LANES + lw))
     u_parts = ((0, 0, LANES, 0), (0, LANES, half, LANES), (1, LANES, half, LANES + half), (1, 0, LANES, 2 * LANES))
 
     def load_attn(l, place, sem):
         for j in range(g.ncol):
-            for f, r0, n, off in q_parts:
-                pltpu.make_async_copy(wq_in.at[l, f, pl.ds(r0, n), pl.ds(j * LANES, LANES)], place(g.q0 + j * 4 * lw + off, n), sem).start()
+            for f in range(4):
+                pltpu.make_async_copy(wq_in.at[l, f, :, pl.ds(j * LANES, LANES)], place(g.q0 + (j * 4 + f) * lw, lw), sem).start()
+
+    def load_bias(l):
+        for h in range(g.heads):
+            pltpu.make_async_copy(bias_in.at[l, h], abuf.at[h, :, pl.ds(0, T)], s_bias).start()
+
+    def turn_bias(l, put):
+        for h in range(g.heads):
+            wait_like(abuf.at[h, :, pl.ds(0, T)], s_bias)
         for h in range(g.heads):
             for j in range(g.tcol):
-                pltpu.make_async_copy(bias_in.at[l, h, :, pl.ds(j * LANES, LANES)], place(g.b0 + (h * g.tcol + j) * T, T), sem).start()
+                put(g.b0 + (h * g.tcol + j) * T, abuf[h, pl.ds(j * LANES, LANES), pl.ds(0, T)].T)
 
     def load_rest(l, place, sem):
         for j in range(g.ncol):
@@ -140,6 +146,7 @@
     def own_rows(l):
         return lambda off, n: buf.at[x, pl.ds(l * g.lr - g.o0 + off, n)]
 
+    load_bias(0)
     load_rest(0, own_rows(0), s_loc.at[1])
     act_cp = pltpu.make_async_copy(act_in.at[pl.ds(mine, own)], abuf, s_act.at[0])
     cond_cp = pltpu.make_async_copy(cond_in.at[pl.ds(mine, own)], cbuf, s_act.at[1])
@@ -169,21 +176,21 @@
 
     def stage1(k):
         await_quarters(2, ra.at[k])
-        push(xm, k, g0, dev_p, rd.at[k])
         for blk in (xm, xp):
             push(blk, k, g0, dev_y, rb.at[k])
             push(blk, k, g0, dev_z, rb.at[k])
 
     def stage2(k):
         await_quarters(4, rb.at[k])
-        push(xm, k, gy, dev_p, rd.at[k])
-        push(xp, k, gz, dev_m, rd.at[k])
         push(xm, k, gz, dev_y, rc.at[k])
         push(xp, k, gy, dev_z, rc.at[k])
 
     def stage3(k):
         await_quarters(2, rc.at[k])
-        push(xp, k, gd, dev_m, rd.at[k])
+        for part in (g0, gy):
+            push(xm, k, part, dev_p, rd.at[k])
+        for part in (gz, gd):
+            push(xp, k, part, dev_m, rd.at[k])
 
     def stage4(k):
         await_quarters(4, rd.at[k])
@@ -203,14 +210,14 @@
         return -(-(rows_end - g.o0) // CH) + lag
 
     lane = lax.broadcasted_iota(jnp.int32, (1, LANES), 1)
-    mask_add = (mask_in[...].astype(F32) - 1.0) * (1e9 * LOG2E)
     scale2 = LOG2E / math.sqrt(hd)
 
-    def modulated(l, j, cond_ln, act_f32):
+    def modulated(l, j, cond_ln, act_of):
         c_in = (cond_ln * ascale_in[l, pl.ds(j, 1), :]).astype(BF16)
-        gain = jax.nn.sigmoid(dot_nn(c_in, adabuf[l * 2 + j, 0]) + abias_in[l, pl.ds(j, 1), :])
+        gain = dot_nn(c_in, adabuf[l * 2 + j, 0])
         shift = dot_nn(c_in, adabuf[l * 2 + j, 1])
-        return (gain * normed(act_f32) + shift).astype(BF16)
+        act_ln = normed(act_of().astype(F32))
+        return (jax.nn.sigmoid(gain + abias_in[l, pl.ds(j, 1), :]) * act_ln + shift).astype(BF16)
 
     def row_blocks(body):
         for r in range(T // RB):
@@ -218,39 +225,28 @@
 
     def ada_sample(l, j, i):
         def rows_body(rows):
-            xbuf[i, rows, :] = modulated(l, j, lnbuf[i, rows, :], abuf[i, rows, :].astype(F32))
+            xbuf[i, rows, :] = modulated(l, j, lnbuf[i, rows, :], lambda: abuf[i, rows, :])
         row_blocks(rows_body)
         remote(xbuf.at[i], xbuf.at[own + i], sx.at[i], rx.at[i], dev_c).start()
 
     stage0 = 2 * own * nx
 
     def relay_box(v):
-        return xbuf.at[v, :, pl.ds(0, LANES)]
-
-    def sent_part(i):
-        return obuf.at[pl.ds(stage0 + i * g.ncol, g.ncol)]
-
-    def got_part(i):
-        return pbuf.at[pl.ds(i * g.ncol, g.ncol)]
+        return xbuf.at[v, pl.ds(0, lw), pl.ds(0, T)]
 
     def resid_sample(l, j, i, part_of):
         rows = pl.ds(0, T)
         ours = part_of(l, i, rows)
         gate = jax.nn.sigmoid(dot_nn(cbuf[i], zerobuf[l * 2 + j]) + zbias_in[l, pl.ds(j, 1), :])
-        wait_like(got_part(i), rp.at[i])
-        theirs = jnp.concatenate([pbuf[i * g.ncol + v] for v in range(g.ncol)], axis=1)
-        act = (abuf[i].astype(F32) + gate * (ours + theirs.astype(F32)).astype(BF16).astype(F32)).astype(BF16)
+        wait_like(pbuf.at[i], rp.at[i])
+        act = (abuf[i].astype(F32) + gate * (ours + pbuf[i].astype(F32)).astype(BF16).astype(F32)).astype(BF16)
         abuf[i] = act
         if j == 1:
             out[mine + i] = act
 
     def part_sample(l, i, part_of):
-        def rows_body(rows):
-            part = part_of(l, own + i, rows).astype(BF16)
-            for v in range(g.ncol):
-                obuf[stage0 + i * g.ncol + v, rows, :] = part[:, v * LANES:(v + 1) * LANES]
-        row_blocks(rows_body)
-        remote(sent_part(i), got_part(i), sp.at[i], rp.at[i], dev_c).start()
+        sbuf[i] = part_of(l, own + i, pl.ds(0, T)).astype(BF16)
+        remote(sbuf.at[i], pbuf.at[i], sp.at[i], rp.at[i], dev_c).start()
 
     def flat(s, l, off, n):
         return buf[s, pl.ds(pl.multiple_of(l * g.lr - g.o0 + off, 8), n), :]
@@ -259,30 +255,47 @@
         for h in range(g.heads):
             for j in range(g.tcol):
                 col = pl.ds(j * LANES, LANES)
-                bmbuf[h, :, col] = rows_of(g.b0 + (h * g.tcol + j) * T, T).astype(F32) * LOG2E + mask_add[:, j * LANES:(j + 1) * LANES]
+                bmbuf[h, :, col] = rows_of(g.b0 + (h * g.tcol + j) * T, T).astype(F32) * LOG2E + mcol[...]
+
+    def project_dot(x_rows, rows_of):
+        w = jnp.concatenate([rows_of(g.q0 + j * 4 * lw, 4 * lw) for j in range(g.ncol)], axis=1)
+        return dot_nt(w, x_rows)
+
+    def project_end(slot, proj, q_bias):
+        qs, ks, vs, gs = slot
+        qs[...] = (proj[:lw] + q_bias).astype(BF16)
+        ks[...] = proj[lw:2 * lw].astype(BF16).T
+        vs[...] = proj[2 * lw:3 * lw].astype(BF16)
+        gs[...] = jax.nn.sigmoid(proj[3 * lw:])
+
+    def scores(slot, h):
+        qs, ks, _, _ = slot
+        none = jnp.zeros((hd, T), BF16)
+        q = jnp.concatenate([qs[pl.ds(h * hd, hd), :] if v == h else none for v in range(g.heads)], axis=0)
+        return dot_nn(ks[...], q)
+
+    def weights(h, s):
+        z = s * scale2 + bmbuf[h]
+        return jnp.exp2(z - jnp.max(z, axis=0, keepdims=True)).astype(BF16)
+
+    def mix(slot, h, e, o_ref):
+        _, _, vs, gs = slot
+        mine_h = pl.ds(h * hd, hd)
+        o = dot_nn(jnp.concatenate([vs[mine_h, :], jnp.ones((16, T), BF16)], axis=0), e)
+        o_ref[mine_h, :] = (o[:hd] * (1.0 / o[hd:hd + 1]) * gs[mine_h, :]).astype(BF16)
 
     def project(slot, x_rows, rows_of, q_bias):
-        qs, ks, vs, gs = slot
-        w = jnp.concatenate([rows_of(g.q0 + j * 4 * lw, 4 * lw) for j in range(g.ncol)], axis=1)
-        proj = dot_nt(x_rows, w)
-        pa, pb, pc = (proj[:, v * LANES:(v + 1) * LANES] for v in range(3))
-        qs[...] = (pa + q_bias).astype(BF16)
-        ks[...] = pb.astype(BF16)
-        vs[...] = jnp.where(lane < lw, pc, 1.0).astype(BF16)
-        gate = jnp.where(lane < 32, pltpu.roll(pa, 32, 1), jnp.where(lane < 64, pltpu.roll(pb, 64, 1), pltpu.roll(pc, 96, 1)))
-        gs[...] = jnp.where(lane < lw, jax.nn.sigmoid(gate), 0.0)
-
-    def attend(slot, o_ref):
-        qs, ks, vs, gs = slot
-        q = qs[...]
-        zero = jnp.zeros((), BF16)
-        both = jnp.concatenate([jnp.where((lane >= h * hd) & (lane < (h + 1) * hd), q, zero) for h in range(g.heads)], axis=0)
-        z = dot_nt(both, ks[...]) * scale2 + jnp.concatenate([bmbuf[h] for h in range(g.heads)], axis=0)
-        e = jnp.exp2(z - jnp.max(z, axis=-1, keepdims=True)).astype(BF16)
-        o = dot_nn(e, vs[...])
-        o = o * (1.0 / o[:, lw:lw + 1])
-        o_ref[...] = (jnp.where(lane < hd, o[:T], o[T:]) * gs[...]).astype(BF16)
-
+        project_end(slot, project_dot(x_rows, rows_of), q_bias)
+
+    def pair(slot, o_ref, after, x_rows, rows_of, q_bias):
+        s0 = scores(slot, 0)
+        s1 = scores(slot, 1)
+        proj = project_dot(x_rows, rows_of)
+        e0 = weights(0, s0)
+        mix(slot, 0, e0, o_ref)
+        e1 = weights(1, s1)
+        mix(slot, 1, e1, o_ref)
+        project_end(after, proj, q_bias)
     slot_a = (qa, ka, va, ga)
     slot_b = (qb, kb, vb, gb)
 
@@ -292,7 +305,7 @@
         wait_like(hbuf.at[slot], s_in.at[0, slot])
         wait_like(cring.at[slot], s_in.at[1, slot])
         def rows_body(rows):
-            out[s, rows, :] = modulated(0, 0, normed(cring[slot, rows, :].astype(F32)), hbuf[slot, rows, :].astype(F32))
+            out[s, rows, :] = modulated(0, 0, normed(cring[slot, rows, :].astype(F32)), lambda: hbuf[slot, rows, :])
         row_blocks(rows_body)
         remote(out.at[s], out.at[s], sx0, rx0.at[n], dev_c).start()
         @pl.when(n + 2 * own < steps)
@@ -308,7 +321,7 @@
         load_sample(n)
     load_attn(1, own_rows(1), s_loc.at[2])
     load_rest(1, own_rows(1), s_loc.at[2])
-    for cp in (cond_cp, act_cp, zero_cps[0], *ada_cps[1:], *zero_cps[1:]):
+    for cp in (cond_cp, zero_cps[0], *ada_cps[1:], *zero_cps[1:]):
         cp.start()
     pl.semaphore_wait(barrier, len(devs))
     wait_like(buf.at[x, pl.ds(0, g.lr - g.o0)], s_loc.at[1])
@@ -316,17 +329,32 @@
     for k in range(min(LA, early)):
         first(k)
     ada_first(0)
-    wait_like(qb0, s_loc.at[0])
+    mask_col = jnp.broadcast_to((mask_in[...].astype(F32) - 1.0) * (1e9 * LOG2E), (8, T)).T
+    mcol[...] = jnp.broadcast_to(mask_col[:, 0:1], (T, LANES))
+
+    def put_first(off, v):
+        qb0[pl.ds(off, T), :] = v
+    turn_bias(0, put_first)
+    load_bias(1)
+    wait_like(qb0.at[pl.ds(0, g.b0)], s_loc.at[0])
     bias_prep(qb_rows)
     for d in (dev_p, dev_m, dev_o):
         remote(bqbuf.at[x], bqbuf.at[x], s_bq, r_bq, d).start()
-    q_bias0 = bqbuf[x, pl.ds(0, 1), :]
+    q_bias0 = bqbuf[x].T[:lw, 0:1]
     project(slot_a, out[sample_of(0, c)], qb_rows, q_bias0)
-    wait_like(buf.at[x, pl.ds(0, g.lr)], s_loc.at[2])
+    wait_like(buf.at[x, pl.ds(0, g.lr - g.o0 + g.b0)], s_loc.at[2])
     for k in range(min(LA, early), LA):
         first(k)
 
+    def put_second(off, v):
+        buf[x, pl.ds(g.lr - g.o0 + off, T), :] = v
+
     def first_steps(m, carry):
+        @pl.when(m == 1)
+        def _():
+            turn_bias(1, put_second)
+            act_cp.start()
+
         @pl.when(m + 1 < steps)
         def _():
             ada_first(m + 1)
@@ -357,21 +385,19 @@
                 wait_like(r, r_rel.at[pair * CORES + u])
                 remote(r, obuf.at[slot_of(pair, core) * nx + source], s_o, r_o, dev).start()
 
-        @pl.when(m == own)
+        @pl.when(m == own + 1)
         def _():
             forward(0, dev_p, xm)
 
-        @pl.when(m == own + 1)
+        @pl.when(m == own + 2)
         def _():
             forward(1, dev_m, xp)
         wait_like(out.at[0], rx0.at[m])
         slot, place = place_of(0, c)
-        attend(slot_a, obuf.at[place])
-        project(slot_b, out[sample_of(m, 1 - c)], qb_rows, q_bias0)
+        pair(slot_a, obuf.at[place], slot_b, out[sample_of(m, 1 - c)], qb_rows, q_bias0)
         send(0, slot, place)
         slot, place = place_of(1, 1 - c)
-        attend(slot_b, obuf.at[place])
-        project(slot_a, out[sample_of(jnp.minimum(m + 1, steps - 1), c)], qb_rows, q_bias0)
+        pair(slot_b, obuf.at[place], slot_a, out[sample_of(jnp.minimum(m + 1, steps - 1), c)], qb_rows, q_bias0)
         send(1, slot, place)
 
         @pl.when(m >= HELD)
@@ -392,19 +418,20 @@
     wait_like(out.at[pl.ds(0, steps)], sx0)
 
     def attn_part(l, i, rows):
-        lhs = jnp.concatenate([obuf[i * nx + s, rows, :] for s in range(nx)], axis=1)
-        zpad = jnp.zeros((LANES - lw, LANES), BF16)
-        rhs = jnp.concatenate([jnp.concatenate([v for s in range(nx) for v in (flat(s, l, g.o0 + j * lw, lw), zpad)], axis=0) for j in range(g.ncol)], axis=1)
-        return dot_nn(lhs, rhs)
+        lhs = jnp.concatenate([obuf[i * nx + s] for s in range(nx)], axis=0)
+        rhs = jnp.concatenate([jnp.concatenate([flat(s, l, g.o0 + j * lw, lw) for s in range(nx)], axis=0) for j in range(g.ncol)], axis=1)
+        return lax.dot_general(lhs, rhs, (((0,), (0,)), ((), ())), preferred_element_type=F32)
 
     def up_sample(l, i):
         y = xbuf[i]
+        pre = []
         for p in range(nx // 2):
             w = jnp.concatenate([jnp.concatenate([flat(2 * p + e, l, g.u0 + j * 2 * hu, 2 * hu) for j in range(g.ncol)], axis=1) for e in range(2)], axis=0)
-            u = dot_nt(y, w)
+            pre.append(dot_nt(y, w))
+        for p in range(nx // 2):
             mids = []
             for e in range(2):
-                ua, ub, uc = (u[:, (3 * e + v) * LANES:(3 * e + v + 1) * LANES] for v in range(3))
+                ua, ub, uc = (pre[p][:, (3 * e + v) * LANES:(3 * e + v + 1) * LANES] for v in range(3))
                 side = (3 * p + 2 * e) * LANES
                 hbuf[i, :, side:side + LANES] = (jax.nn.silu(ua) * uc).astype(BF16)
                 act = jax.nn.silu(ub)
@@ -452,7 +479,8 @@
 
     t0 = steps - HELD
     t1 = t0 + TAIL_TICKS
-    assert K + LAGS[-1] <= t1 + nx * own and need(g.lr, LAGS[-1]) <= t0 + 4
+    assert K + LAGS[-1] <= t1 + nx and need(g.d0, LAGS[-1]) <= t0 + 2 and need(g.lr, LAGS[-1]) <= t0 + 4
+    assert need(g.lr + g.o0, LAGS[-1]) <= t1 + nx - 1 and need(g.lr + g.o0, LAGS[2]) <= t1
 
     def arrived(lo, hi):
         for k in range(lo, hi):
@@ -472,13 +500,12 @@
     @each(own)
     def _(i):
         part_sample(0, i, attn_part)
-    tick(t0)
 
     @each(own)
     def _(i):
         resid_sample(0, 0, i, attn_part)
         ada_sample(0, 1, i)
-        tick(t0 + 1 + i)
+        tick(t0 + i)
     arrived(k_o, k_u)
 
     @each(2 * own)
@@ -490,12 +517,12 @@
 
         @pl.when(lax.rem(i, 2) == 1)
         def _():
-            tick(t0 + 3 + i // 2)
+            tick(t0 + 2 + i // 2)
     arrived(k_u, k_d)
 
     @each(own)
     def _(i):
-        wait_like(sent_part(0), sp.at[i])
+        wait_like(sbuf.at[0], sp.at[i])
         part_sample(0, i, trans_part)
         wait_like(xbuf.at[0], sx.at[i])
 
@@ -503,7 +530,10 @@
     def _(i):
         resid_sample(0, 1, i, trans_part)
         ada_sample(1, 0, i)
-        tick(t0 + 5 + i)
+
+        @pl.when(i < TAIL_TICKS - 4)
+        def _():
+            tick(t0 + 4 + i)
     wait_like(bqbuf.at[pl.ds(0, nx - 1)], r_bq)
 
     k_q, k_o, k_u, k_d = (need(g.lr + v, 0) for v in (g.o0, g.u0, g.d0, g.lr))
@@ -516,7 +546,7 @@
         return lambda off, n: flat(s, 1, off, n)
 
     def q_bias1(s):
-        return bqbuf[s, pl.ds(1, 1), :]
+        return bqbuf[s].T[:lw, 1:2]
 
     def half_layer(hf, carry):
         def once(body):
@@ -529,35 +559,32 @@
             s = shard_of(q)
             after = shard_of(jnp.minimum(q + 1, nx - 1))
             bias_prep(rows_from(s))
-            pl.when((hf > 0) & (q == RELAY_AT))(lambda: out_relay(0))
-            attend(slot_a, obuf.at[hf * nx + s])
-            project(slot_b, xbuf[own + hf], rows_from(s), q_bias1(s))
+            pair(slot_a, obuf.at[hf * nx + s], slot_b, xbuf[own + hf], rows_from(s), q_bias1(s))
 
             @pl.when(hf == 0)
             def _():
-                tick(t1 + 2 * q)
+                tick(t1 + q)
 
                 @pl.when(q == nx - 2)
                 def _():
                     arrived(first_k, k_q)
-            attend(slot_b, obuf.at[(own + hf) * nx + s])
-            project(slot_a, xbuf[hf], rows_from(after), q_bias1(after))
-            once(lambda: tick(t1 + 2 * q + 1))
+            pair(slot_b, obuf.at[(own + hf) * nx + s], slot_a, xbuf[hf], rows_from(after), q_bias1(after))
             return inner
         lax.fori_loop(0, nx, shard, 0)
         once(lambda: arrived(k_q, k_o))
-        wait_like(sent_part(hf), sp.at[hf])
+        pl.when(hf > 0)(lambda: out_relay(0))
+        wait_like(sbuf.at[hf], sp.at[hf])
         part_sample(1, hf, attn_part)
         wait_like(xbuf.at[hf], sx.at[hf])
         resid_sample(1, 0, hf, attn_part)
         ada_sample(1, 1, hf)
         once(lambda: arrived(k_o, k_u))
+        up_sample(1, hf)
         pl.when(hf > 0)(lambda: out_relay(1))
-        up_sample(1, hf)
         wait_like(xbuf.at[own + hf], rx.at[hf])
         up_sample(1, own + hf)
         once(lambda: arrived(k_u, k_d))
-        wait_like(sent_part(hf), sp.at[hf])
+        wait_like(sbuf.at[hf], sp.at[hf])
         part_sample(1, hf, trans_part)
         resid_sample(1, 1, hf, trans_part)
         out_first(hf)
@@ -566,7 +593,7 @@
     lax.fori_loop(0, own, half_layer, 0)
     for i in range(own):
         wait_like(xbuf.at[i], sx.at[i])
-        wait_like(sent_part(i), sp.at[i])
+        wait_like(sbuf.at[i], sp.at[i])
     for p in range(npc, own * npc):
         out_relay(p)
     for p in range(own * npc):
@@ -609,8 +636,9 @@
                 pltpu.VMEM((g.o0, LANES), BF16),
                 pltpu.VMEM((2 * own, T, D), BF16),
                 pltpu.VMEM((own, T, D), BF16),
-                pltpu.VMEM((own * g.ncol, T, LANES), BF16),
-                pltpu.VMEM((2 * own * nx + own * g.ncol, T, LANES), BF16),
+                pltpu.VMEM((own, T, D), BF16),
+                pltpu.VMEM((own, T, D), BF16),
+                pltpu.VMEM((2 * own * nx + CORES * (steps - own), g.lw, T), BF16),
                 pltpu.VMEM((2 * own, T, nx * g.hu), BF16),
                 pltpu.VMEM((2 * own, T, C), BF16),
                 pltpu.VMEM((own, T, C), BF16),
@@ -618,16 +646,17 @@
                 pltpu.VMEM((2 * L, 2, C, D), BF16),
                 pltpu.VMEM((2 * L, C, D), BF16),
                 pltpu.VMEM((nx, 8, LANES), F32),
+                pltpu.VMEM((T, LANES), F32),
                 pltpu.VMEM((g.heads, T, T), F32),
-                pltpu.VMEM((T, LANES), BF16),
-                pltpu.VMEM((T, LANES), BF16),
-                pltpu.VMEM((T, LANES), BF16),
-                pltpu.VMEM((T, LANES), F32),
-                pltpu.VMEM((T, LANES), BF16),
-                pltpu.VMEM((T, LANES), BF16),
-                pltpu.VMEM((T, LANES), BF16),
-                pltpu.VMEM((T, LANES), F32),
-                dma((3,)), dma((3,)), dma((4 * L,)), dma((2, 2 * own)), dma,
+                pltpu.VMEM((g.lw, T), BF16),
+                pltpu.VMEM((T, g.lw), BF16),
+                pltpu.VMEM((g.lw, T), BF16),
+                pltpu.VMEM((g.lw, T), F32),
+                pltpu.VMEM((g.lw, T), BF16),
+                pltpu.VMEM((T, g.lw), BF16),
+                pltpu.VMEM((g.lw, T), BF16),
+                pltpu.VMEM((g.lw, T), F32),
+                dma((3,)), dma((3,)), dma, dma((4 * L,)), dma((2, 2 * own)), dma,
                 dma((K,)), dma((K,)), dma((K,)), dma((K,)),
                 dma, dma, dma, dma((steps,)), dma, dma, dma((CORES * own,)),
                 dma((own,)), dma((own,)), dma((own,)), dma((own,)),

time: 190 us -> 162 us (0.85)
  Pallas kernels: 184 us -> 155 us
    pallas_call x1, Pallas kernels: 179 us -> 151 us  [body(): pl.pallas_call(functools.partial(kernel, g), out_shape=pltpu.VMEM(token_a...]
where the time goes in v4:
time: 162 us
  Pallas kernels  155 us (96%)
  local copies, waits for them, and re-layouts  6.35 us (4%)
    pallas_call x1, Pallas kernels, body(): pl.pallas_call(functools.partial(kernel, g), out_shape=pltpu.VMEM(token_a...  151 us
    pallas_call x1, Pallas kernels, body(): pl.pallas_call(finish, out_shape=jax.ShapeDtypeStruct(token_act.shape, BF...  4.79 us
    transpose x1, local copies, waits for them, and re-layouts, body(): zero = zero_w.transpose(0, 2, 1, 3).reshape(2 * L, C, D)  3.52 us

profile of v4, /device:TPU:81, one launch (start us, length us, event | category | flops | bytes accessed | tf_op | source)
XLA Modules:
  0.0 161.9 jit_solution(8012157895730349124)
XLA Ops:
  0.0 0.0 copy-start
  0.0 3.5 %copy.16 = bf16[2,2,384,768]{3,2,1,0:T(8,128)(2,1)} copy(bf16[2,2,384,768]{3,1,2,0:T(2,128)(2,1)} %bitcast.10) | data formatting | bytes 4718592 | tf_op jit(solution)/shard_map/transpose | solution.py:622
  3.5 0.0 copy-done
  3.5 2.8 %copy.15 = bf16[2,2,2,384,768]{4,3,2,1,0:T(8,128)(2,1)} copy(bf16[2,2,2,384,768]{4,2,3,1,0:T(2,128)(2,1)S(1)} %bitcast.9) | data formatting | bytes 9437184 | tf_op jit(solution)/shard_map/transpose | solution.py:621
  6.3 150.6 %blocks.1.src = bf16[16,512,768]{2,1,0:T(8,128)(2,1)S(1)} custom-call(bf16[16,512,768]{2,1,0:T(8,128)(2,1)} %act_in.1, bf16[16,512,384]{2,1,0:T(8,128)(2,1)} %cond_in.1, bf16[2,2,512,512]{3,2,1,0:T(8,128)(2,1)} %bias_in.1, s32[1,512]{1,0:T(1,128)} %bitcast.13, f32[2,2,384]{2,1,0:T(2,128)} %ascale_in.1, bf16[4,2,384,768]{3,2,1,0:T(8,128)(2,1)} %bitcast.7, ...), custom_call_target="tpu_custom_call" | custom-call | tf_op jit(solution)/shard_map/blocks/pallas_call | solution.py:629
  157.0 4.8 %finish.1 = bf16[16,512,768]{2,1,0:T(8,128)(2,1)} custom-call(bf16[16,512,768]{2,1,0:T(8,128)(2,1)S(1)} %blocks.1.src), custom_call_target="tpu_custom_call" | custom-call | tf_op jit(solution)/shard_map/finish/pallas_call | solution.py:669
Async XLA Ops:
  0.0 3.5 %copy-start = (bf16[2,2,384,2,768]{4,3,2,1,0:T(2,128)(2,1)S(1)}, bf16[2,2,384,2,768]{4,3,2,1,0:T(2,128)(2,1)}, u32[]{:S(2)}) copy-start(bf16[2,2,384,2,768]{4,3,2,1,0:T(2,128)(2,1)} %param.19) | copy-start | bytes 14155780

commit v5 on v4

--- a/solution.py
+++ b/solution.py
@@ -17,10 +17,12 @@
 LA = 4
 TAIL_TICKS = 6
 HELD = 0
+EARLY_LAG = 4
 LAGS = (0, 2, 5)
 RB = 512
 OUT_ROWS = 256
 CORES = 2
+RING = 2
 
 
 def dot_nt(lhs, rhs):
@@ -108,7 +110,7 @@
         return chip_of(n) * (CORES * own) + pair_of(n) * CORES + core
 
     def load_sample(n):
-        slot = lax.rem(n, 2 * own)
+        slot = lax.rem(n, RING)
         pltpu.make_async_copy(act_in.at[sample_of(n, c)], hbuf.at[slot], s_in.at[0, slot]).start()
         pltpu.make_async_copy(cond_in.at[sample_of(n, c)], cring.at[slot], s_in.at[1, slot]).start()
 
@@ -201,8 +203,9 @@
         @pl.when(t + LA < K)
         def _():
             first(t + LA)
-        for lag, stage in zip(LAGS, (stage1, stage2, stage3)):
-            @pl.when((t >= lag) & (t - lag < K))
+        split = need(g.lr, 0)
+        for lag, stage, lo, hi in ((LAGS[0], stage1, 0, K), (LAGS[1], stage2, 0, K), (EARLY_LAG, stage3, 0, split), (LAGS[2], stage3, split, K)):
+            @pl.when((t - lag >= lo) & (t - lag < hi))
             def _(lag=lag, stage=stage):
                 stage(t - lag)
 
@@ -214,39 +217,37 @@
 
     def modulated(l, j, cond_ln, act_of):
         c_in = (cond_ln * ascale_in[l, pl.ds(j, 1), :]).astype(BF16)
-        gain = dot_nn(c_in, adabuf[l * 2 + j, 0])
+        gain = jax.nn.sigmoid(dot_nn(c_in, adabuf[l * 2 + j, 0]) + abias_in[l, pl.ds(j, 1), :])
         shift = dot_nn(c_in, adabuf[l * 2 + j, 1])
-        act_ln = normed(act_of().astype(F32))
-        return (jax.nn.sigmoid(gain + abias_in[l, pl.ds(j, 1), :]) * act_ln + shift).astype(BF16)
+        return (gain * normed(act_of().astype(F32)) + shift).astype(BF16)
 
     def row_blocks(body):
         for r in range(T // RB):
             body(pl.ds(r * RB, RB))
 
-    def ada_sample(l, j, i):
-        def rows_body(rows):
-            xbuf[i, rows, :] = modulated(l, j, lnbuf[i, rows, :], lambda: abuf[i, rows, :])
-        row_blocks(rows_body)
-        remote(xbuf.at[i], xbuf.at[own + i], sx.at[i], rx.at[i], dev_c).start()
+    full = pl.ds(0, T)
+
+    def ada_rows(l, j, i, rows, n=0):
+        xbuf[i, rows, :] = modulated(l, j, lnbuf[i, rows, :], lambda: abuf[i, rows, :])
+        remote(xbuf.at[i, rows], xbuf.at[own + i, rows], sx.at[i, n], rx.at[i, n], dev_c).start()
+
+    def resid_rows(l, j, i, part_of, rows, n=0):
+        ours = part_of(l, i, rows)
+        gate = jax.nn.sigmoid(dot_nn(cbuf[i, rows, :], zerobuf[l * 2 + j]) + zbias_in[l, pl.ds(j, 1), :])
+        wait_like(pbuf.at[i, rows], rp.at[i, n])
+        act = (abuf[i, rows, :].astype(F32) + gate * (ours + pbuf[i, rows, :].astype(F32)).astype(BF16).astype(F32)).astype(BF16)
+        abuf[i, rows, :] = act
+        if j == 1:
+            out[mine + i, rows, :] = act
+
+    def part_rows(l, i, part_of, rows, n=0):
+        sbuf[i, rows, :] = part_of(l, own + i, rows).astype(BF16)
+        remote(sbuf.at[i, rows], pbuf.at[i, rows], sp.at[i, n], rp.at[i, n], dev_c).start()
 
     stage0 = 2 * own * nx
 
     def relay_box(v):
         return xbuf.at[v, pl.ds(0, lw), pl.ds(0, T)]
-
-    def resid_sample(l, j, i, part_of):
-        rows = pl.ds(0, T)
-        ours = part_of(l, i, rows)
-        gate = jax.nn.sigmoid(dot_nn(cbuf[i], zerobuf[l * 2 + j]) + zbias_in[l, pl.ds(j, 1), :])
-        wait_like(pbuf.at[i], rp.at[i])
-        act = (abuf[i].astype(F32) + gate * (ours + pbuf[i].astype(F32)).astype(BF16).astype(F32)).astype(BF16)
-        abuf[i] = act
-        if j == 1:
-            out[mine + i] = act
-
-    def part_sample(l, i, part_of):
-        sbuf[i] = part_of(l, own + i, pl.ds(0, T)).astype(BF16)
-        remote(sbuf.at[i], pbuf.at[i], sp.at[i], rp.at[i], dev_c).start()
 
     def flat(s, l, off, n):
         return buf[s, pl.ds(pl.multiple_of(l * g.lr - g.o0 + off, 8), n), :]
@@ -300,7 +301,7 @@
     slot_b = (qb, kb, vb, gb)
 
     def ada_first(n):
-        slot = lax.rem(n, 2 * own)
+        slot = lax.rem(n, RING)
         s = sample_of(n, c)
         wait_like(hbuf.at[slot], s_in.at[0, slot])
         wait_like(cring.at[slot], s_in.at[1, slot])
@@ -308,16 +309,16 @@
             out[s, rows, :] = modulated(0, 0, normed(cring[slot, rows, :].astype(F32)), lambda: hbuf[slot, rows, :])
         row_blocks(rows_body)
         remote(out.at[s], out.at[s], sx0, rx0.at[n], dev_c).start()
-        @pl.when(n + 2 * own < steps)
-        def _():
-            load_sample(n + 2 * own)
+        @pl.when(n + RING < steps)
+        def _():
+            load_sample(n + RING)
 
     def qb_rows(off, n):
         return qb0[pl.ds(off, n), :]
 
     ada_cps[0].wait()
     load_attn(0, lambda off, n: qb0.at[pl.ds(off, n)], s_loc.at[0])
-    for n in range(1, 2 * own):
+    for n in range(1, RING):
         load_sample(n)
     load_attn(1, own_rows(1), s_loc.at[2])
     load_rest(1, own_rows(1), s_loc.at[2])
@@ -418,12 +419,12 @@
     wait_like(out.at[pl.ds(0, steps)], sx0)
 
     def attn_part(l, i, rows):
-        lhs = jnp.concatenate([obuf[i * nx + s] for s in range(nx)], axis=0)
+        lhs = jnp.concatenate([obuf[i * nx + s, :, rows] for s in range(nx)], axis=0)
         rhs = jnp.concatenate([jnp.concatenate([flat(s, l, g.o0 + j * lw, lw) for s in range(nx)], axis=0) for j in range(g.ncol)], axis=1)
         return lax.dot_general(lhs, rhs, (((0,), (0,)), ((), ())), preferred_element_type=F32)
 
-    def up_sample(l, i):
-        y = xbuf[i]
+    def up_rows(l, i, rows=full):
+        y = xbuf[i, rows, :]
         pre = []
         for p in range(nx // 2):
             w = jnp.concatenate([jnp.concatenate([flat(2 * p + e, l, g.u0 + j * 2 * hu, 2 * hu) for j in range(g.ncol)], axis=1) for e in range(2)], axis=0)
@@ -433,11 +434,11 @@
             for e in range(2):
                 ua, ub, uc = (pre[p][:, (3 * e + v) * LANES:(3 * e + v + 1) * LANES] for v in range(3))
                 side = (3 * p + 2 * e) * LANES
-                hbuf[i, :, side:side + LANES] = (jax.nn.silu(ua) * uc).astype(BF16)
+                hbuf[i, rows, side:side + LANES] = (jax.nn.silu(ua) * uc).astype(BF16)
                 act = jax.nn.silu(ub)
                 mids.append(act * pltpu.roll(ub, half, 1) if e == 0 else pltpu.roll(act, half, 1) * ub)
             mid = (3 * p + 1) * LANES
-            hbuf[i, :, mid:mid + LANES] = jnp.where(lane < half, mids[0], mids[1]).astype(BF16)
+            hbuf[i, rows, mid:mid + LANES] = jnp.where(lane < half, mids[0], mids[1]).astype(BF16)
 
     def trans_part(l, i, rows):
         cols = []
@@ -463,12 +464,10 @@
     def oawait(halves, sem):
         wait_like(out.at[0, pl.ds(0, halves * PR // 2)], sem)
 
-    def out_first(i):
-        for h in range(npc):
-            p = i * npc + h
-            opush(orow(tp, p), dev_p, o_a.at[p])
-            opush(orow(tp, p), dev_m, o_a.at[p])
-            opush(orow(tp, p), dev_c, o_p0.at[p])
+    def out_first(p):
+        opush(orow(tp, p), dev_p, o_a.at[p])
+        opush(orow(tp, p), dev_m, o_a.at[p])
+        opush(orow(tp, p), dev_c, o_p0.at[p])
 
     def out_relay(p):
         oawait(4, o_a.at[p])
@@ -499,12 +498,12 @@
 
     @each(own)
     def _(i):
-        part_sample(0, i, attn_part)
+        part_rows(0, i, attn_part, full)
 
     @each(own)
     def _(i):
-        resid_sample(0, 0, i, attn_part)
-        ada_sample(0, 1, i)
+        resid_rows(0, 0, i, attn_part, full)
+        ada_rows(0, 1, i, full)
         tick(t0 + i)
     arrived(k_o, k_u)
 
@@ -512,8 +511,8 @@
     def _(i):
         @pl.when(i >= own)
         def _():
-            wait_like(xbuf.at[0], rx.at[i - own])
-        up_sample(0, i)
+            wait_like(xbuf.at[0], rx.at[i - own, 0])
+        up_rows(0, i)
 
         @pl.when(lax.rem(i, 2) == 1)
         def _():
@@ -522,14 +521,14 @@
 
     @each(own)
     def _(i):
-        wait_like(sbuf.at[0], sp.at[i])
-        part_sample(0, i, trans_part)
-        wait_like(xbuf.at[0], sx.at[i])
+        wait_like(sbuf.at[0], sp.at[i, 0])
+        part_rows(0, i, trans_part, full)
+        wait_like(xbuf.at[0], sx.at[i, 0])
 
     @each(own)
     def _(i):
-        resid_sample(0, 1, i, trans_part)
-        ada_sample(1, 0, i)
+        resid_rows(0, 1, i, trans_part, full)
+        ada_rows(1, 0, i, full)
 
         @pl.when(i < TAIL_TICKS - 4)
         def _():
@@ -553,12 +552,13 @@
             pl.when(hf == 0)(body)
 
         project(slot_a, xbuf[hf], rows_from(x), q_bias1(x))
-        wait_like(xbuf.at[own + hf], rx.at[hf])
+        wait_like(xbuf.at[own + hf], rx.at[hf, 0])
 
         def shard(q, inner):
             s = shard_of(q)
             after = shard_of(jnp.minimum(q + 1, nx - 1))
             bias_prep(rows_from(s))
+            pl.when((hf > 0) & (q == nx - 1))(lambda: out_relay(0))
             pair(slot_a, obuf.at[hf * nx + s], slot_b, xbuf[own + hf], rows_from(s), q_bias1(s))
 
             @pl.when(hf == 0)
@@ -572,28 +572,38 @@
             return inner
         lax.fori_loop(0, nx, shard, 0)
         once(lambda: arrived(k_q, k_o))
-        pl.when(hf > 0)(lambda: out_relay(0))
-        wait_like(sbuf.at[hf], sp.at[hf])
-        part_sample(1, hf, attn_part)
-        wait_like(xbuf.at[hf], sx.at[hf])
-        resid_sample(1, 0, hf, attn_part)
-        ada_sample(1, 1, hf)
+        ha, hb = (pl.ds(v * PR, PR) for v in range(2))
+        wait_like(sbuf.at[hf], sp.at[hf, 0])
+        wait_like(xbuf.at[hf], sx.at[hf, 0])
+        part_rows(1, hf, attn_part, ha, 0)
+        part_rows(1, hf, attn_part, hb, 1)
+        resid_rows(1, 0, hf, attn_part, ha, 0)
+        ada_rows(1, 1, hf, ha, 0)
         once(lambda: arrived(k_o, k_u))
-        up_sample(1, hf)
+        up_rows(1, hf, ha)
+        resid_rows(1, 0, hf, attn_part, hb, 1)
+        ada_rows(1, 1, hf, hb, 1)
+        wait_like(xbuf.at[own + hf, ha], rx.at[hf, 0])
+        up_rows(1, own + hf, ha)
+        once(lambda: arrived(k_u, k_d))
+        wait_like(sbuf.at[hf, ha], sp.at[hf, 0])
+        part_rows(1, hf, trans_part, ha, 0)
+        up_rows(1, hf, hb)
         pl.when(hf > 0)(lambda: out_relay(1))
-        wait_like(xbuf.at[own + hf], rx.at[hf])
-        up_sample(1, own + hf)
-        once(lambda: arrived(k_u, k_d))
-        wait_like(sbuf.at[hf], sp.at[hf])
-        part_sample(1, hf, trans_part)
-        resid_sample(1, 1, hf, trans_part)
-        out_first(hf)
+        resid_rows(1, 1, hf, trans_part, ha, 0)
+        out_first(hf * npc)
+        wait_like(xbuf.at[own + hf, hb], rx.at[hf, 1])
+        up_rows(1, own + hf, hb)
+        wait_like(sbuf.at[hf, hb], sp.at[hf, 1])
+        part_rows(1, hf, trans_part, hb, 1)
+        resid_rows(1, 1, hf, trans_part, hb, 1)
+        out_first(hf * npc + 1)
+        for n, rows in enumerate((ha, hb)):
+            wait_like(xbuf.at[hf, rows], sx.at[hf, n])
+            wait_like(sbuf.at[hf, rows], sp.at[hf, n])
         return carry
 
     lax.fori_loop(0, own, half_layer, 0)
-    for i in range(own):
-        wait_like(xbuf.at[i], sx.at[i])
-        wait_like(sbuf.at[i], sp.at[i])
     for p in range(npc, own * npc):
         out_relay(p)
     for p in range(own * npc):
@@ -609,9 +619,11 @@
 
 
 def finish(src, dst, sem):
-    cp = pltpu.make_async_copy(src, dst, sem)
-    cp.start()
-    cp.wait()
+    cps = [pltpu.make_async_copy(src.at[v], dst.at[v], sem.at[v]) for v in range(src.shape[0])]
+    for cp in cps:
+        cp.start()
+    for cp in cps:
+        cp.wait()
 
 
 def solution(mesh):
@@ -640,7 +652,7 @@
                 pltpu.VMEM((own, T, D), BF16),
                 pltpu.VMEM((2 * own * nx + CORES * (steps - own), g.lw, T), BF16),
                 pltpu.VMEM((2 * own, T, nx * g.hu), BF16),
-                pltpu.VMEM((2 * own, T, C), BF16),
+                pltpu.VMEM((RING, T, C), BF16),
                 pltpu.VMEM((own, T, C), BF16),
                 pltpu.VMEM((own, T, C), F32),
                 pltpu.VMEM((2 * L, 2, C, D), BF16),
@@ -656,10 +668,10 @@
                 pltpu.VMEM((T, g.lw), BF16),
                 pltpu.VMEM((g.lw, T), BF16),
                 pltpu.VMEM((g.lw, T), F32),
-                dma((3,)), dma((3,)), dma, dma((4 * L,)), dma((2, 2 * own)), dma,
+                dma((3,)), dma((3,)), dma, dma((4 * L,)), dma((2, RING)), dma,
                 dma((K,)), dma((K,)), dma((K,)), dma((K,)),
                 dma, dma, dma, dma((steps,)), dma, dma, dma((CORES * own,)),
-                dma((own,)), dma((own,)), dma((own,)), dma((own,)),
+                dma((own, 2)), dma((own, 2)), dma((own, 2)), dma((own, 2)),
                 dma, dma((npc,)), dma((npc,)), dma((npc,)), dma((npc,)), dma((npc,)),
             ],
             compiler_params=pltpu.CompilerParams(collective_id=0, has_side_effects=True, vmem_limit_bytes=207 << 18),
@@ -671,7 +683,7 @@
             out_shape=jax.ShapeDtypeStruct(token_act.shape, BF16),
             in_specs=[vm],
             out_specs=pl.BlockSpec(memory_space=pltpu.HBM),
-            scratch_shapes=[dma],
+            scratch_shapes=[dma((token_act.shape[0],))],
             compiler_params=pltpu.CompilerParams(vmem_limit_bytes=1 << 20),
             name='finish',
         )(gathered)

time: 162 us -> 159 us (0.981)
  Pallas kernels: 155 us -> 152 us
    pallas_call x1, Pallas kernels: 151 us -> 148 us  [body(): pl.pallas_call(functools.partial(kernel, g), out_shape=pltpu.VMEM(token_a...]
where the time goes in v5:
time: 159 us
  Pallas kernels  152 us (96%)
  local copies, waits for them, and re-layouts  6.35 us (4%)
    pallas_call x1, Pallas kernels, body(): pl.pallas_call(functools.partial(kernel, g), out_shape=pltpu.VMEM(token_a...  148 us
    pallas_call x1, Pallas kernels, body(): pl.pallas_call(finish, out_shape=jax.ShapeDtypeStruct(token_act.shape, BF...  4.7 us
    transpose x1, local copies, waits for them, and re-layouts, body(): zero = zero_w.transpose(0, 2, 1, 3).reshape(2 * L, C, D)  3.52 us

profile of v5, /device:TPU:81, one launch (start us, length us, event | category | flops | bytes accessed | tf_op | source)
XLA Modules:
  0.0 158.7 jit_solution(8553959258410783177)
XLA Ops:
  0.0 0.0 copy-start
  0.0 3.5 %copy.16 = bf16[2,2,384,768]{3,2,1,0:T(8,128)(2,1)} copy(bf16[2,2,384,768]{3,1,2,0:T(2,128)(2,1)} %bitcast.10) | data formatting | bytes 4718592 | tf_op jit(solution)/shard_map/transpose | solution.py:634
  3.5 0.0 copy-done
  3.5 2.8 %copy.15 = bf16[2,2,2,384,768]{4,3,2,1,0:T(8,128)(2,1)} copy(bf16[2,2,2,384,768]{4,2,3,1,0:T(2,128)(2,1)S(1)} %bitcast.9) | data formatting | bytes 9437184 | tf_op jit(solution)/shard_map/transpose | solution.py:633
  6.3 147.5 %blocks.1.src = bf16[16,512,768]{2,1,0:T(8,128)(2,1)S(1)} custom-call(bf16[16,512,768]{2,1,0:T(8,128)(2,1)} %act_in.1, bf16[16,512,384]{2,1,0:T(8,128)(2,1)} %cond_in.1, bf16[2,2,512,512]{3,2,1,0:T(8,128)(2,1)} %bias_in.1, s32[1,512]{1,0:T(1,128)} %bitcast.13, f32[2,2,384]{2,1,0:T(2,128)} %ascale_in.1, bf16[4,2,384,768]{3,2,1,0:T(8,128)(2,1)} %bitcast.7, ...), custom_call_target="tpu_custom_call" | custom-call | tf_op jit(solution)/shard_map/blocks/pallas_call | solution.py:641
  153.9 4.7 %finish.1 = bf16[16,512,768]{2,1,0:T(8,128)(2,1)} custom-call(bf16[16,512,768]{2,1,0:T(8,128)(2,1)S(1)} %blocks.1.src), custom_call_target="tpu_custom_call" | custom-call | tf_op jit(solution)/shard_map/finish/pallas_call | solution.py:681
Async XLA Ops:
  0.0 3.5 %copy-start = (bf16[2,2,384,2,768]{4,3,2,1,0:T(2,128)(2,1)S(1)}, bf16[2,2,384,2,768]{4,3,2,1,0:T(2,128)(2,1)}, u32[]{:S(2)}) copy-start(bf16[2,2,384,2,768]{4,3,2,1,0:T(2,128)(2,1)} %param.19) | copy-start | bytes 14155780

commit v6 on v5

--- a/solution.py
+++ b/solution.py
@@ -200,14 +200,15 @@
     K = g.chunks
 
     def tick(t):
-        @pl.when(t + LA < K)
-        def _():
-            first(t + LA)
         split = need(g.lr, 0)
-        for lag, stage, lo, hi in ((LAGS[0], stage1, 0, K), (LAGS[1], stage2, 0, K), (EARLY_LAG, stage3, 0, split), (LAGS[2], stage3, split, K)):
+        for lag, stage, lo, hi in ((EARLY_LAG, stage3, 0, split), (LAGS[2], stage3, split, K), (LAGS[0], stage1, 0, K), (LAGS[1], stage2, 0, K)):
             @pl.when((t - lag >= lo) & (t - lag < hi))
             def _(lag=lag, stage=stage):
                 stage(t - lag)
+
+        @pl.when(t + LA < K)
+        def _():
+            first(t + LA)
 
     def need(rows_end, lag):
         return -(-(rows_end - g.o0) // CH) + lag
@@ -300,7 +301,7 @@
     slot_a = (qa, ka, va, ga)
     slot_b = (qb, kb, vb, gb)
 
-    def ada_first(n):
+    def ada_first(n, ready=lambda: None):
         slot = lax.rem(n, RING)
         s = sample_of(n, c)
         wait_like(hbuf.at[slot], s_in.at[0, slot])
@@ -308,6 +309,7 @@
         def rows_body(rows):
             out[s, rows, :] = modulated(0, 0, normed(cring[slot, rows, :].astype(F32)), lambda: hbuf[slot, rows, :])
         row_blocks(rows_body)
+        ready()
         remote(out.at[s], out.at[s], sx0, rx0.at[n], dev_c).start()
         @pl.when(n + RING < steps)
         def _():
@@ -324,12 +326,14 @@
     load_rest(1, own_rows(1), s_loc.at[2])
     for cp in (cond_cp, zero_cps[0], *ada_cps[1:], *zero_cps[1:]):
         cp.start()
-    pl.semaphore_wait(barrier, len(devs))
-    wait_like(buf.at[x, pl.ds(0, g.lr - g.o0)], s_loc.at[1])
     early = (g.lr - g.o0) // CH
-    for k in range(min(LA, early)):
-        first(k)
-    ada_first(0)
+
+    def open_links():
+        pl.semaphore_wait(barrier, len(devs))
+        wait_like(buf.at[x, pl.ds(0, g.lr - g.o0)], s_loc.at[1])
+        for k in range(min(LA, early)):
+            first(k)
+    ada_first(0, open_links)
     mask_col = jnp.broadcast_to((mask_in[...].astype(F32) - 1.0) * (1e9 * LOG2E), (8, T)).T
     mcol[...] = jnp.broadcast_to(mask_col[:, 0:1], (T, LANES))
 
@@ -583,13 +587,13 @@
         up_rows(1, hf, ha)
         resid_rows(1, 0, hf, attn_part, hb, 1)
         ada_rows(1, 1, hf, hb, 1)
+        pl.when(hf > 0)(lambda: out_relay(1))
         wait_like(xbuf.at[own + hf, ha], rx.at[hf, 0])
         up_rows(1, own + hf, ha)
         once(lambda: arrived(k_u, k_d))
         wait_like(sbuf.at[hf, ha], sp.at[hf, 0])
         part_rows(1, hf, trans_part, ha, 0)
         up_rows(1, hf, hb)
-        pl.when(hf > 0)(lambda: out_relay(1))
         resid_rows(1, 1, hf, trans_part, ha, 0)
         out_first(hf * npc)
         wait_like(xbuf.at[own + hf, hb], rx.at[hf, 1])

time: 159 us -> 158 us (level)
  no operation moved by 1% of the time
where the time goes in v6:
time: 158 us
  Pallas kernels  152 us (96%)
  local copies, waits for them, and re-layouts  6.35 us (4%)
    pallas_call x1, Pallas kernels, body(): pl.pallas_call(functools.partial(kernel, g), out_shape=pltpu.VMEM(token_a...  147 us
    pallas_call x1, Pallas kernels, body(): pl.pallas_call(finish, out_shape=jax.ShapeDtypeStruct(token_act.shape, BF...  4.7 us
    transpose x1, local copies, waits for them, and re-layouts, body(): zero = zero_w.transpose(0, 2, 1, 3).reshape(2 * L, C, D)  3.52 us

profile of v6, /device:TPU:81, one launch (start us, length us, event | category | flops | bytes accessed | tf_op | source)
XLA Modules:
  0.0 158.3 jit_solution(17163411085292329520)
XLA Ops:
  0.0 0.0 copy-start
  0.0 3.5 %copy.16 = bf16[2,2,384,768]{3,2,1,0:T(8,128)(2,1)} copy(bf16[2,2,384,768]{3,1,2,0:T(2,128)(2,1)} %bitcast.10) | data formatting | bytes 4718592 | tf_op jit(solution)/shard_map/transpose | solution.py:638
  3.5 0.0 copy-done
  3.5 2.8 %copy.15 = bf16[2,2,2,384,768]{4,3,2,1,0:T(8,128)(2,1)} copy(bf16[2,2,2,384,768]{4,2,3,1,0:T(2,128)(2,1)S(1)} %bitcast.9) | data formatting | bytes 9437184 | tf_op jit(solution)/shard_map/transpose | solution.py:637
  6.3 147.0 %blocks.1.src = bf16[16,512,768]{2,1,0:T(8,128)(2,1)S(1)} custom-call(bf16[16,512,768]{2,1,0:T(8,128)(2,1)} %act_in.1, bf16[16,512,384]{2,1,0:T(8,128)(2,1)} %cond_in.1, bf16[2,2,512,512]{3,2,1,0:T(8,128)(2,1)} %bias_in.1, s32[1,512]{1,0:T(1,128)} %bitcast.13, f32[2,2,384]{2,1,0:T(2,128)} %ascale_in.1, bf16[4,2,384,768]{3,2,1,0:T(8,128)(2,1)} %bitcast.7, ...), custom_call_target="tpu_custom_call" | custom-call | tf_op jit(solution)/shard_map/blocks/pallas_call | solution.py:645
  153.4 4.7 %finish.1 = bf16[16,512,768]{2,1,0:T(8,128)(2,1)} custom-call(bf16[16,512,768]{2,1,0:T(8,128)(2,1)S(1)} %blocks.1.src), custom_call_target="tpu_custom_call" | custom-call | tf_op jit(solution)/shard_map/finish/pallas_call | solution.py:685
Async XLA Ops:
  0.0 3.5 %copy-start = (bf16[2,2,384,2,768]{4,3,2,1,0:T(2,128)(2,1)S(1)}, bf16[2,2,384,2,768]{4,3,2,1,0:T(2,128)(2,1)}, u32[]{:S(2)}) copy-start(bf16[2,2,384,2,768]{4,3,2,1,0:T(2,128)(2,1)} %param.19) | copy-start | bytes 14155780
